TPU v7x, 32 devices: a whole 2x2x4 slice. The times are simulated.
32 devices in a mesh: ma: 16 (over z, y, core), freq: 2 (over x).
Axes of the slice: x: 2, y: 2, z: 4, core: 2. Of those that a mesh axis runs over, the one named last changes fastest.
Arguments:
- right_side: float32 [128, 8, 2, 512], P('ma', 'freq'), may hold values from -60 to 60
- start_field: float32 [128, 8, 2, 512], P('ma', 'freq'), may hold values from -6 to 6
- beam: float32 [128, 8, 2, 16, 512], P('ma', 'freq'), may hold values from -0.75 to 0.75
- noise: float32 [128, 8, 16], P('ma', 'freq'), may hold values from 0.3 to 3
- inv_power: float32 [512], replicated, may hold values from 0.5 to 2
- smooth: float32 [512], replicated, may hold values from 0.5 to 4
Outputs:
- solution_field: float32 [128, 8, 2, 512], P('ma', 'freq')
- residual: float32 [128, 8, 2, 512], P('ma', 'freq')
All inputs are finite; a program needn't handle non-finite values.
Results may differ from a plain program's by a relative error of at most 0.0003.
Values sent between devices are 32-bit elements; how exact they have to be, the bound alone decides.
No kernel may reach another device: no remote copies, remote signals or barrier semaphores. Data moves between devices by JAX's collectives and lax.ppermute only.
A program may use at most 64 MiB of HBM per device.

v0:
```python
import jax
import jax.numpy as jnp
from jax import lax
from jax.sharding import PartitionSpec as P

ITERS = 2


def extended(array, sides, width):
    for axis, dim in sides:
        size, length = (lax.axis_size(axis), array.shape[dim])
        up = [(i, (i + 1) % size) for i in range(size - 1)]
        down = [(j, i) for i, j in up]
        last = lax.slice_in_dim(array, length - width, length, axis=dim)
        leading = lax.slice_in_dim(array, 0, width, axis=dim)
        before = lax.ppermute(last, axis, up)
        after = lax.ppermute(leading, axis, down)
        array = jnp.concatenate([before, array, after], axis=dim)
    return array


def beam_image(field, beam, noise):
    projected = jnp.einsum("mfakl,mfbl->mfabk", beam, field, precision=lax.Precision.HIGHEST)
    real_part = projected[:, :, 0, 0] + projected[:, :, 1, 1]
    imaginary = projected[:, :, 0, 1] - projected[:, :, 1, 0]
    weighted = jnp.stack([real_part, imaginary], axis=2) * noise[:, :, None, :]
    back = jnp.einsum("mfakl,mfbk->mfabl", beam, weighted, precision=lax.Precision.HIGHEST)
    return jnp.stack(
        [back[:, :, 0, 0] - back[:, :, 1, 1], back[:, :, 0, 1] + back[:, :, 1, 0]], axis=2
    )


def prior_term(padded, field, first, total, smooth):
    channel = first + jnp.arange(field.shape[1], dtype=jnp.int32)
    weight = (channel > 0).astype(jnp.float32) + (channel < total - 1).astype(jnp.float32)
    return smooth * (weight[None, :, None, None] * field - padded[:, :-2] - padded[:, 2:])


def two_products(vector, applied):
    return lax.psum((jnp.sum(vector * vector), jnp.sum(vector * applied)), ("ma", "freq"))


def shards(right_side, start_field, beam, noise, inv_power, smooth):
    first = lax.axis_index("freq") * right_side.shape[1]
    total = right_side.shape[1] * lax.axis_size("freq")

    def padded_of(field):
        return extended(field, (("freq", 1),), 1)

    def operate(field):
        prior = prior_term(padded_of(field), field, first, total, smooth)
        return beam_image(field, beam, noise) + inv_power * field + prior

    solution = start_field
    resid_now = right_side - operate(start_field)
    applied = operate(resid_now)
    norm_now, curve_now = two_products(resid_now, applied)
    step_size = norm_now / curve_now
    direction = resid_now
    along = applied
    for turn in range(ITERS):
        solution = solution + step_size * direction
        resid_now = resid_now - step_size * along
        if turn + 1 < ITERS:
            applied = operate(resid_now)
            norm_next, curve_now = two_products(resid_now, applied)
            growth = norm_next / norm_now
            step_size = norm_next / (curve_now - growth * norm_next / step_size)
            direction = resid_now + growth * direction
            along = applied + growth * along
            norm_now = norm_next
    return (solution, resid_now)


def solution(mesh):
    in_specs = (
        P("ma", "freq", None, None),
        P("ma", "freq", None, None),
        P("ma", "freq", None, None, None),
        P("ma", "freq", None),
        P(),
        P(),
    )
    out_specs = (P("ma", "freq", None, None), P("ma", "freq", None, None))
    return jax.shard_map(shards, mesh=mesh, in_specs=in_specs, out_specs=out_specs, check_vma=False)
```

profile of v0, /device:TPU:0, one launch (start us, length us, event | category | flops | bytes accessed | tf_op | source)
XLA Modules:
  0.0 144.0 jit_solution(10948142598104500641)
XLA Ops:
  0.6 0.0 copy-start
  0.7 0.9 fusion.42
  1.6 4.9 %collective-permute-start = (f32[8,1,2,512]{3,2,1,0:T(2,128)S(1)}, f32[8,1,2,512]{3,2,1,0:T(2,128)S(1)}, u32[]{:S(2)}, u32[]{:S(2)}) collective-permute-start(f32[8,1,2,512]{3,2,1,0:T(2,128)S(1)} %get-tuple-element.22), channel_id=1, source_target_pairs={{0,1},{2,3},{4,5},{6,7},{8,9},{10,11},{12,13},{14,15},{16,17},{18,... | collective-permute-start | bytes 98312 | tf_op jit(solution)/shard_map/ppermute | solution.py:16
  6.5 1.3 collective-permute-start.1
  7.8 8.3 %convolution_bitcast_fusion.1 = f32[8,4,2,2,16]{4,3,2,1,0:T(2,128)S(1)} fusion(f32[8,4,2,16,512]{4,3,2,1,0:T(8,128)S(1)} %copy-done, f32[8,4,2,512]{3,2,1,0:T(2,128)} %param.7), kind=kOutput, calls=%fused_computation.1 | convolution fusion | flops 12582912 | bytes 2236416 | tf_op jit(solution)/shard_map/mfakl,mfbl->mfabk/dot_general | solution.py:23
  16.1 0.0 copy-start.4
  16.1 0.0 copy-start.5
  16.2 1.1 convolution_bitcast_fusion
  17.3 0.1 fusion.22
  17.4 0.1 fusion.24
  17.6 0.3 fusion.11
  17.9 7.4 %fusion.15 = f32[8,4,2,2,16]{4,2,3,1,0:T(2,128)S(1)} fusion(f32[8,4,2,16,512]{4,3,2,1,0:T(8,128)S(1)} %copy-done, f32[8,4,2,512]{3,2,1,0:T(2,128)S(1)} %fusion.11), kind=kOutput, calls=%fused_computation.28 | convolution fusion | flops 12582912 | bytes 2236416 | tf_op jit(solution)/shard_map/mfakl,mfbl->mfabk/dot_general | solution.py:23
  25.4 1.3 fusion.30
  26.7 0.1 copy.46
  26.9 4.5 %collective-permute-start.2 = (f32[8,1,2,512]{3,2,1,0:T(2,128)S(1)}, f32[8,1,2,512]{3,2,1,0:T(2,128)S(1)}, u32[]{:S(2)}, u32[]{:S(2)}) collective-permute-start(f32[8,1,2,512]{3,2,1,0:T(2,128)S(1)} %get-tuple-element.20), channel_id=1, source_target_pairs={{0,1},{2,3},{4,5},{6,7},{8,9},{10,11},{12,13},{14,15},{16,17},{18,... | collective-permute-start | bytes 98312 | tf_op jit(solution)/shard_map/ppermute | solution.py:16
  31.4 1.3 collective-permute-start.3
  32.7 0.1 fusion.21
  32.9 0.1 collective-permute-done.2
  33.0 4.2 %collective-permute-done.3 = f32[8,1,2,512]{3,2,1,0:T(2,128)S(1)} collective-permute-done((f32[8,1,2,512]{3,2,1,0:T(2,128)S(1)}, f32[8,1,2,512]{3,2,1,0:T(2,128)S(1)}, u32[]{:S(2)}, u32[]{:S(2)}) %collective-permute-start.3) | collective-permute-done | bytes 32800 | tf_op jit(solution)/shard_map/ppermute | solution.py:17
  37.2 1.1 multiply_reduce_fusion.2
  38.3 39.8 %all-reduce.1 = (f32[]{:T(128)}, f32[]{:T(128)}) all-reduce(f32[]{:T(128)} %get-tuple-element.5, f32[]{:T(128)} %get-tuple-element.4), channel_id=1, replica_groups=mesh['ma'=16,'freq'=2] {'ma','freq'}, use_global_device_ids=true, to_apply=%region_1.0 | all-reduce | flops 2 | bytes 16 | tf_op jit(solution)/shard_map/psum | solution.py:40
  79.4 7.4 %fusion.13 = f32[8,4,2,2,16]{4,2,3,1,0:T(2,128)S(1)} fusion(f32[8,4,2,16,512]{4,3,2,1,0:T(8,128)S(1)} %copy-done, f32[8,4,2,512]{3,2,1,0:T(2,128)S(1)} %bitcast.90), kind=kOutput, calls=%fused_computation.26 | convolution fusion | flops 12582912 | bytes 2236416 | tf_op jit(solution)/shard_map/mfakl,mfbl->mfabk/dot_general | solution.py:23
  86.9 1.1 fusion.28
  88.0 0.1 copy.45
  88.2 4.2 %collective-permute-start.4 = (f32[8,1,2,512]{3,2,1,0:T(2,128)S(1)}, f32[8,1,2,512]{3,2,1,0:T(2,128)S(1)}, u32[]{:S(2)}, u32[]{:S(2)}) collective-permute-start(f32[8,1,2,512]{3,2,1,0:T(2,128)S(1)} %get-tuple-element.18), channel_id=1, source_target_pairs={{0,1},{2,3},{4,5},{6,7},{8,9},{10,11},{12,13},{14,15},{16,17},{18,... | collective-permute-start | bytes 98312 | tf_op jit(solution)/shard_map/ppermute | solution.py:16
  92.4 1.3 collective-permute-start.5
  93.7 0.1 fusion.19
  93.8 0.1 collective-permute-done.4
  93.9 4.2 %collective-permute-done.5 = f32[8,1,2,512]{3,2,1,0:T(2,128)S(1)} collective-permute-done((f32[8,1,2,512]{3,2,1,0:T(2,128)S(1)}, f32[8,1,2,512]{3,2,1,0:T(2,128)S(1)}, u32[]{:S(2)}, u32[]{:S(2)}) %collective-permute-start.5) | collective-permute-done | bytes 32800 | tf_op jit(solution)/shard_map/ppermute | solution.py:17
  98.2 1.1 multiply_reduce_fusion
  99.3 39.4 %all-reduce = (f32[]{:T(128)}, f32[]{:T(128)}) all-reduce(f32[]{:T(128)} %get-tuple-element.3, f32[]{:T(128)} %get-tuple-element.2), channel_id=1, replica_groups=mesh['ma'=16,'freq'=2] {'ma','freq'}, use_global_device_ids=true, to_apply=%region_5.0 | all-reduce | flops 2 | bytes 16 | tf_op jit(solution)/shard_map/psum | solution.py:40
  143.3 0.8 multiply_subtract_fusion
  (24 shorter events, 0.2 us)
Async XLA Ops:
  0.6 7.1 %copy-start = (f32[8,4,2,16,512]{4,3,2,1,0:T(8,128)S(1)}, f32[8,4,2,16,512]{4,3,2,1,0:T(8,128)}, u32[]{:S(2)}) copy-start(f32[8,4,2,16,512]{4,3,2,1,0:T(8,128)} %param.8) | copy-start | bytes 6291460
  0.6 15.5 %copy-start.2 = (f32[8,4,16]{2,1,0:T(4,128)S(1)}, f32[8,4,16]{2,1,0:T(4,128)}, u32[]{:S(2)}) copy-start(f32[8,4,16]{2,1,0:T(4,128)} %param.9) | copy-start | bytes 6148
  1.6 16.0 %collective-permute-start = (f32[8,1,2,512]{3,2,1,0:T(2,128)S(1)}, f32[8,1,2,512]{3,2,1,0:T(2,128)S(1)}, u32[]{:S(2)}, u32[]{:S(2)}) collective-permute-start(f32[8,1,2,512]{3,2,1,0:T(2,128)S(1)} %get-tuple-element.22), channel_id=1, source_target_pairs={{0,1},{2,3},{4,5},{6,7},{8,9},{10,11},{12,13},{14,15},{16,17},{18,... | collective-permute-start | bytes 98312 | tf_op jit(solution)/shard_map/ppermute | solution.py:16
  6.5 11.1 %collective-permute-start.1 = (f32[8,1,2,512]{3,2,1,0:T(2,128)S(1)}, f32[8,1,2,512]{3,2,1,0:T(2,128)S(1)}, u32[]{:S(2)}, u32[]{:S(2)}) collective-permute-start(f32[8,1,2,512]{3,2,1,0:T(2,128)S(1)} %get-tuple-element.23), channel_id=1, source_target_pairs={{1,0},{3,2},{5,4},{7,6},{9,8},{11,10},{13,12},{15,14},{17,16},{19,... | collective-permute-start | bytes 98312 | tf_op jit(solution)/shard_map/ppermute | solution.py:17
  16.1 1.5 %copy-start.1 = (f32[8,4,2,512]{3,2,1,0:T(2,128)S(1)}, f32[8,4,2,512]{3,2,1,0:T(2,128)}, u32[]{:S(2)}) copy-start(f32[8,4,2,512]{3,2,1,0:T(2,128)} %param.7) | copy-start | bytes 393220
  16.1 1.5 %copy-start.3 = (f32[8,4,2,512]{3,2,1,0:T(2,128)S(1)}, f32[8,4,2,512]{3,2,1,0:T(2,128)}, u32[]{:S(2)}) copy-start(f32[8,4,2,512]{3,2,1,0:T(2,128)} %param.6) | copy-start | bytes 393220
  16.1 1.6 %copy-start.4 = (f32[512]{0:T(512)S(1)}, f32[512]{0:T(512)}, u32[]{:S(2)}) copy-start(f32[512]{0:T(512)} %param.11) | copy-start | bytes 6148
  16.1 1.5 %copy-start.5 = (f32[512]{0:T(512)S(1)}, f32[512]{0:T(512)}, u32[]{:S(2)}) copy-start(f32[512]{0:T(512)} %param.10) | copy-start | bytes 6148
  26.9 6.1 %collective-permute-start.2 = (f32[8,1,2,512]{3,2,1,0:T(2,128)S(1)}, f32[8,1,2,512]{3,2,1,0:T(2,128)S(1)}, u32[]{:S(2)}, u32[]{:S(2)}) collective-permute-start(f32[8,1,2,512]{3,2,1,0:T(2,128)S(1)} %get-tuple-element.20), channel_id=1, source_target_pairs={{0,1},{2,3},{4,5},{6,7},{8,9},{10,11},{12,13},{14,15},{16,17},{18,... | collective-permute-start | bytes 98312 | tf_op jit(solution)/shard_map/ppermute | solution.py:16
  31.4 5.8 %collective-permute-start.3 = (f32[8,1,2,512]{3,2,1,0:T(2,128)S(1)}, f32[8,1,2,512]{3,2,1,0:T(2,128)S(1)}, u32[]{:S(2)}, u32[]{:S(2)}) collective-permute-start(f32[8,1,2,512]{3,2,1,0:T(2,128)S(1)} %get-tuple-element.21), channel_id=1, source_target_pairs={{1,0},{3,2},{5,4},{7,6},{9,8},{11,10},{13,12},{15,14},{17,16},{19,... | collective-permute-start | bytes 98312 | tf_op jit(solution)/shard_map/ppermute | solution.py:17
  88.2 5.8 %collective-permute-start.4 = (f32[8,1,2,512]{3,2,1,0:T(2,128)S(1)}, f32[8,1,2,512]{3,2,1,0:T(2,128)S(1)}, u32[]{:S(2)}, u32[]{:S(2)}) collective-permute-start(f32[8,1,2,512]{3,2,1,0:T(2,128)S(1)} %get-tuple-element.18), channel_id=1, source_target_pairs={{0,1},{2,3},{4,5},{6,7},{8,9},{10,11},{12,13},{14,15},{16,17},{18,... | collective-permute-start | bytes 98312 | tf_op jit(solution)/shard_map/ppermute | solution.py:16
  92.4 5.8 %collective-permute-start.5 = (f32[8,1,2,512]{3,2,1,0:T(2,128)S(1)}, f32[8,1,2,512]{3,2,1,0:T(2,128)S(1)}, u32[]{:S(2)}, u32[]{:S(2)}) collective-permute-start(f32[8,1,2,512]{3,2,1,0:T(2,128)S(1)} %get-tuple-element.19), channel_id=1, source_target_pairs={{1,0},{3,2},{5,4},{7,6},{9,8},{11,10},{13,12},{15,14},{17,16},{19,... | collective-permute-start | bytes 98312 | tf_op jit(solution)/shard_map/ppermute | solution.py:17
where the time goes:
time: 145 us; the launch traced here: 144 us
  blocking collectives  79.2 us (55%)
  matrix products  26.7 us (18%)
  starting transfers between devices  17.5 us (12%)
  waiting for transfers between devices  8.73 us (6%)
  between operations  6.85 us (5%)
  other arithmetic  3.86 us (3%)
    psum x2, blocking collectives, two_products(): lax.psum((jnp.sum(vector * vector), jnp.sum(vector * applied)), ('ma', 'f...  79.2 us
    dot_general x3, matrix products, beam_image(): jnp.einsum('mfakl,mfbl->mfabk', beam, field, precision=lax.Precision.HIGH...  23.1 us
    ppermute x3, starting transfers between devices, extended(): before = lax.ppermute(last, axis, up)  13.6 us
    ppermute x3, waiting for transfers between devices, extended(): after = lax.ppermute(leading, axis, down)  8.46 us
    ppermute x3, starting transfers between devices, extended(): after = lax.ppermute(leading, axis, down)  3.88 us
    dot_general x3, matrix products, beam_image(): jnp.einsum('mfakl,mfbk->mfabl', beam, weighted, precision=lax.Precision.H...  3.6 us
  transfers between devices with their start and end apart: 6, of which 4 were waited for; matrix products, arithmetic and copies ran while one was open for 7% of the time, Pallas kernels for 0%

commit v1 on v0

v1 whole, which is shorter than its diff:
```python
import jax
import jax.numpy as jnp
from jax import lax
from jax.experimental import pallas as pl
from jax.experimental.pallas import tpu as pltpu
from jax.sharding import PartitionSpec as P

AXES = ("ma", "freq")
LANES = 128
VMEM_LIMIT = 12 * 1024 * 1024


def column(row):
    size = row.shape[1]
    spread = jnp.broadcast_to(row, (size, size))
    diagonal = lax.broadcasted_iota(jnp.int32, (size, size), 0) == lax.broadcasted_iota(
        jnp.int32, (size, size), 1
    )
    return jnp.sum(jnp.where(diagonal, spread, 0.0), axis=1, keepdims=True)


def stacked(real, imaginary):
    shape = (2, real.shape[1])
    first = lax.broadcasted_iota(jnp.int32, shape, 0) == 0
    return jnp.where(first, jnp.broadcast_to(real, shape), jnp.broadcast_to(imaginary, shape))


def beam_row(beam_ref, m, f, row, gain):
    real, imaginary = beam_ref[m, f, 0], beam_ref[m, f, 1]
    v_real, v_imag = row[0:1], row[1:2]
    p_real = jnp.sum(real * v_real + imaginary * v_imag, axis=1, keepdims=True) * gain
    p_imag = jnp.sum(real * v_imag - imaginary * v_real, axis=1, keepdims=True) * gain
    back_real = jnp.sum(real * p_real - imaginary * p_imag, axis=0, keepdims=True)
    back_imag = jnp.sum(real * p_imag + imaginary * p_real, axis=0, keepdims=True)
    return stacked(back_real, back_imag)


def counts(index, size, length):
    total = size * length
    out = []
    for f in range(length):
        channel = index * length + f
        out.append(
            jnp.where(channel > 0, 1.0, 0.0) + jnp.where(channel < total - 1, 1.0, 0.0)
        )
    return out


def local_rows(rows, m, beam_ref, noise_ref, inv, smooth, weights):
    out = []
    gains = noise_ref[m]
    for f, row in enumerate(rows):
        prior = weights[f] * row
        if f > 0:
            prior = prior - rows[f - 1]
        if f + 1 < len(rows):
            prior = prior - rows[f + 1]
        image = beam_row(beam_ref, m, f, row, column(gains[f : f + 1]))
        out.append(image + inv * row + smooth * prior)
    return out


def call(body, outs, *args):
    return pl.pallas_call(
        body,
        out_shape=outs,
        compiler_params=pltpu.CompilerParams(vmem_limit_bytes=VMEM_LIMIT),
    )(*args)


def shards(size, devices, right_side, start_field, beam, noise, inv_power, smooth):
    modes, length = right_side.shape[:2]
    width = right_side.shape[3]
    pair = size == 2
    field = jax.ShapeDtypeStruct(right_side.shape, jnp.float32)
    index = lax.axis_index("freq")
    inv_power = inv_power.reshape(1, width)
    smooth = smooth.reshape(1, width)
    up = [(i, i + 1) for i in range(size - 1)]
    down = [(j, i) for i, j in up]

    def exchanged(sends):
        if pair:
            return [lax.ppermute(sends[0], "freq", up + down)]
        return [lax.ppermute(sends[0], "freq", up), lax.ppermute(sends[1], "freq", down)]

    def edges(first, last, at):
        return [jnp.where(at == 0, last, first)] if pair else [last, first]

    def masks():
        at = lax.axis_index("freq")
        return at, jnp.where(at > 0, 1.0, 0.0), jnp.where(at < size - 1, 1.0, 0.0)

    def sides(values, below, above):
        low, high = (values[0], values[0]) if pair else (values[0], values[1])
        return low * below, high * above

    starts = exchanged(edges(start_field[:, 0], start_field[:, length - 1], index))

    def first(x_ref, b_ref, beam_ref, noise_ref, inv_ref, smooth_ref, p_ref):
        at, _, _ = masks()
        inv, strength = inv_ref[...], smooth_ref[...]
        weights = counts(at, size, length)

        def step(m, _):
            rows = [x_ref[m, f] for f in range(length)]
            images = local_rows(rows, m, beam_ref, noise_ref, inv, strength, weights)
            for f in range(length):
                p_ref[m, f] = b_ref[m, f] - images[f]
            return 0

        lax.fori_loop(0, modes, step, 0)

    partial = call(first, field, start_field, right_side, beam, noise, inv_power, smooth)

    ways = len(starts)
    send = jax.ShapeDtypeStruct((2, modes, 2, width), jnp.float32)

    def second(*refs):
        halo_refs, refs = refs[:ways], refs[ways:]
        p_ref, beam_ref, noise_ref, inv_ref, smooth_ref, r_ref, q_ref = refs[:7]
        send_refs = refs[7:]
        at, below, above = masks()
        inv, strength = inv_ref[...], smooth_ref[...]
        weights = counts(at, size, length)

        def step(m, _):
            low, high = sides([h[m] for h in halo_refs], below, above)
            rows = [p_ref[m, f] for f in range(length)]
            rows[0] = rows[0] + strength * low
            rows[-1] = rows[-1] + strength * high
            images = local_rows(rows, m, beam_ref, noise_ref, inv, strength, weights)
            for f in range(length):
                r_ref[m, f] = rows[f]
                q_ref[m, f] = images[f]
            for ref, r_edge, q_edge in zip(
                send_refs, edges(rows[0], rows[-1], at), edges(images[0], images[-1], at)
            ):
                ref[0, m] = r_edge
                ref[1, m] = q_edge
            return 0

        lax.fori_loop(0, modes, step, 0)

    resid, image, *sends = call(
        second, (field, field) + (send,) * ways, *starts, partial, beam, noise, inv_power, smooth
    )
    halos = exchanged(sends)

    def third(*refs):
        halo_refs, refs = refs[:ways], refs[ways:]
        r_ref, q_ref, beam_ref, noise_ref, inv_ref, smooth_ref, w_ref, z_ref, sums_ref = refs
        at, below, above = masks()
        inv, strength = inv_ref[...], smooth_ref[...]
        weights = counts(at, size, length)

        def step(m, sums):
            r_low, r_high = sides([h[0, m] for h in halo_refs], below, above)
            q_low, q_high = sides([h[1, m] for h in halo_refs], below, above)
            resids = [r_ref[m, f] for f in range(length)]
            rows = [q_ref[m, f] for f in range(length)]
            rows[0] = rows[0] - strength * r_low
            rows[-1] = rows[-1] - strength * r_high
            images = local_rows(rows, m, beam_ref, noise_ref, inv, strength, weights)
            images[0] = images[0] - strength * (q_low - below * strength * resids[0])
            images[-1] = images[-1] - strength * (q_high - above * strength * resids[-1])
            rr, rw, ww, wz = sums
            for f in range(length):
                w_ref[m, f] = rows[f]
                z_ref[m, f] = images[f]
                rr = rr + resids[f] * resids[f]
                rw = rw + resids[f] * rows[f]
                ww = ww + rows[f] * rows[f]
                wz = wz + rows[f] * images[f]
            return rr, rw, ww, wz

        zero = jnp.zeros((2, width), jnp.float32)
        sums = lax.fori_loop(0, modes, step, (zero, zero, zero, zero))
        lane = lax.broadcasted_iota(jnp.int32, (1, LANES), 1)
        packed = jnp.zeros((1, LANES), jnp.float32)
        for at_lane, value in enumerate(sums):
            packed = jnp.where(lane == at_lane, jnp.sum(value), packed)
        sums_ref[...] = jnp.broadcast_to(packed, (devices, LANES))

    along, twice, sums = call(
        third,
        (field, field, jax.ShapeDtypeStruct((devices, LANES), jnp.float32)),
        *halos, resid, image, beam, noise, inv_power, smooth,
    )
    sums = lax.all_to_all(sums, AXES, 0, 0, tiled=True)

    def last(sums_ref, x_ref, r_ref, w_ref, z_ref, out_ref, resid_ref):
        total = jnp.sum(sums_ref[...], axis=0, keepdims=True)
        lane = lax.broadcasted_iota(jnp.int32, (1, LANES), 1)
        rr, rw, ww, wz = [
            jnp.sum(jnp.where(lane == i, total, 0.0), axis=1, keepdims=True) for i in range(4)
        ]
        step0 = rr / rw
        cross = rw - step0 * ww
        rr1 = rr - 2.0 * step0 * rw + step0 * step0 * ww
        growth = rr1 / rr
        curve = rw - 2.0 * step0 * ww + step0 * step0 * wz + growth * cross
        step1 = rr1 / curve
        on_r = (step0 + step1 * (1.0 + growth)).reshape(1, 1, 1, 1)
        on_w = (step1 * step0).reshape(1, 1, 1, 1)
        r, w = r_ref[...], w_ref[...]
        out_ref[...] = x_ref[...] + on_r * r - on_w * w
        resid_ref[...] = r - on_r * w + on_w * z_ref[...]

    return tuple(call(last, (field, field), sums, start_field, resid, along, twice))


def solution(mesh):
    size, devices = mesh.shape["freq"], mesh.size

    def body(*args):
        return shards(size, devices, *args)

    in_specs = (
        P("ma", "freq", None, None),
        P("ma", "freq", None, None),
        P("ma", "freq", None, None, None),
        P("ma", "freq", None),
        P(),
        P(),
    )
    out_specs = (P("ma", "freq", None, None), P("ma", "freq", None, None))
    return jax.shard_map(body, mesh=mesh, in_specs=in_specs, out_specs=out_specs, check_vma=False)
```

time: 145 us -> 32 us (0.22)
  blocking collectives: 79.2 us -> 12 us
  matrix products: 26.7 us -> 0 us
  starting transfers between devices: 17.5 us -> 3.11 us
  between operations: 6.85 us -> 0.68 us
  Pallas kernels: 0 us -> 5.03 us
  waiting for transfers between devices: 8.73 us -> 4.25 us
  local copies, waits for them, and re-layouts: 1.29 us -> 5.77 us
  other arithmetic: 3.86 us -> 0.8 us
    psum x2 -> x0, blocking collectives: 79.2 us -> none  [two_products(): lax.psum((jnp.sum(vector * vector), jnp.sum(vector * applied)), ('ma', 'f...]
    dot_general x6 -> x0, matrix products: 26.7 us -> none  [the longest x3 23.1 us: beam_image(): jnp.einsum('mfakl,mfbl->mfabk', beam, field, precision=lax.Precision.HIGH...]
    ppermute x6 -> x2, starting transfers between devices: 17.5 us -> 3.11 us  [exchanged(): return [lax.ppermute(sends[0], 'freq', up + down)]]
    all_to_all x0 -> x1, blocking collectives: none -> 12 us  [shards(): sums = lax.all_to_all(sums, AXES, 0, 0, tiled=True)]
    unnamed x12 -> x16, local copies, waits for them, and re-layouts: 0.04 us -> 5.77 us
    pallas_call x0 -> x4, Pallas kernels: none -> 5.03 us  [call(): pl.pallas_call(body, out_shape=outs, compiler_params=pltpu.CompilerParams...]
    ppermute x6 -> x2, waiting for transfers between devices: 8.73 us -> 4.25 us  [exchanged(): return [lax.ppermute(sends[0], 'freq', up + down)]]
    reduce_sum x2 -> x0, other arithmetic: 2.2 us -> none  [two_products(): jnp.sum(vector * applied)]
  transfers between devices with their start and end apart: 6 -> 2, of which waited for: 4 -> 1; matrix products, arithmetic and copies ran while one was open for 7% -> 0% of each run, Pallas kernels for 0% -> 4%
where the time goes in v1:
time: 32 us; the launch traced here: 31.6 us
  blocking collectives  12 us (38%)
  local copies, waits for them, and re-layouts  5.77 us (18%)
  Pallas kernels  5.03 us (16%)
  waiting for transfers between devices  4.25 us (13%)
  starting transfers between devices  3.11 us (10%)
  other arithmetic  0.8 us (2%)
  between operations  0.68 us (2%)
    all_to_all x1, blocking collectives, shards(): sums = lax.all_to_all(sums, AXES, 0, 0, tiled=True)  12 us
    unnamed x16, local copies, waits for them, and re-layouts  5.77 us
    pallas_call x4, Pallas kernels, call(): pl.pallas_call(body, out_shape=outs, compiler_params=pltpu.CompilerParams...  5.03 us
    ppermute x2, waiting for transfers between devices, exchanged(): return [lax.ppermute(sends[0], 'freq', up + down)]  4.25 us
    ppermute x2, starting transfers between devices, exchanged(): return [lax.ppermute(sends[0], 'freq', up + down)]  3.11 us
    select_n x1, other arithmetic, edges(): return [jnp.where(at == 0, last, first)] if pair else [last, first]  0.8 us
  transfers between devices with their start and end apart: 2, of which 1 were waited for; matrix products, arithmetic and copies ran while one was open for 0% of the time, Pallas kernels for 4%

profile of v1, /device:TPU:0, one launch (start us, length us, event | category | flops | bytes accessed | tf_op | source)
XLA Modules:
  0.0 31.6 jit_solution(11536467785652534161)
XLA Ops:
  0.6 0.8 %fusion = f32[8,2,512]{2,1,0:T(2,128)S(1)} fusion(f32[8,4,2,512]{3,2,1,0:T(2,128)} %x_ref.3, pred[]{:T(512)S(6)} %eq.3), kind=kLoop, calls=%fused_computation.1 | loop fusion | flops 8192 | bytes 98305 | tf_op jit(solution)/shard_map/jit(_where)/select_n | solution.py:88
  1.4 3.0 %collective-permute-start = (f32[8,2,512]{2,1,0:T(2,128)S(1)}, f32[8,2,512]{2,1,0:T(2,128)S(1)}, u32[]{:S(2)}, u32[]{:S(2)}) collective-permute-start(f32[8,2,512]{2,1,0:T(2,128)S(1)} %fusion), channel_id=1, source_target_pairs={{0,1},{1,0},{2,3},{3,2},{4,5},{5,4},{6,7},{7,6},{8,9},{9,8},{10,11... | collective-permute-start | bytes 98312 | tf_op jit(solution)/shard_map/ppermute | solution.py:84
  4.5 0.0 copy-start
  4.5 1.6 %copy-done = f32[8,4,2,16,512]{4,3,2,1,0:T(8,128)S(1)} copy-done((f32[8,4,2,16,512]{4,3,2,1,0:T(8,128)S(1)}, f32[8,4,2,16,512]{4,3,2,1,0:T(8,128)}, u32[]{:S(2)}) %copy-start) | copy-done | bytes 2097176
  6.1 0.0 copy-start.2
  6.1 0.9 %copy-done.2 = f32[8,4,2,512]{3,2,1,0:T(2,128)S(1)} copy-done((f32[8,4,2,512]{3,2,1,0:T(2,128)S(1)}, f32[8,4,2,512]{3,2,1,0:T(2,128)}, u32[]{:S(2)}) %copy-start.2) | copy-done | bytes 131096
  7.0 0.0 copy-start.3
  7.0 0.7 %copy-done.3 = f32[8,4,16]{2,1,0:T(4,128)S(1)} copy-done((f32[8,4,16]{2,1,0:T(4,128)S(1)}, f32[8,4,16]{2,1,0:T(4,128)}, u32[]{:S(2)}) %copy-start.3) | copy-done | bytes 2072
  7.7 0.0 copy-start.5
  7.7 0.9 %copy-done.5 = f32[8,4,2,512]{3,2,1,0:T(2,128)S(1)} copy-done((f32[8,4,2,512]{3,2,1,0:T(2,128)S(1)}, f32[8,4,2,512]{3,2,1,0:T(2,128)}, u32[]{:S(2)}) %copy-start.5) | copy-done | bytes 131096
  8.6 0.0 copy-start.6
  8.6 0.7 %copy-done.6 = f32[512]{0:T(512)S(1)} copy-done((f32[512]{0:T(512)S(1)}, f32[512]{0:T(512)}, u32[]{:S(2)}) %copy-start.6) | copy-done | bytes 2072
  9.3 0.0 copy-start.7
  9.3 0.7 %copy-done.7 = f32[512]{0:T(512)S(1)} copy-done((f32[512]{0:T(512)S(1)}, f32[512]{0:T(512)}, u32[]{:S(2)}) %copy-start.7) | copy-done | bytes 2072
  9.9 0.0 copy-start.1
  10.0 0.0 copy-start.4
  10.0 1.3 %shard_map.77.refs_1_ = f32[8,4,2,512]{3,2,1,0:T(2,128)S(1)} custom-call(f32[8,4,2,512]{3,2,1,0:T(2,128)S(1)} %copy-done.2, f32[8,4,2,512]{3,2,1,0:T(2,128)S(1)} %copy-done.5, f32[8,4,2,16,512]{4,3,2,1,0:T(8,128)S(1)} %copy-done, f32[8,4,16]{2,1,0:T(4,128)S(1)} %copy-done.3, f32[1,512]{1,0:T(1,128)S(1)} %bitcast.15, f32[1,512]{1,0:T(1,128)S(1)} %bitcast.18), custom_call_target="tpu_custom_call" | custom-call | tf_op jit(solution)/shard_map/pallas_call | solution.py:64
  11.2 0.0 collective-permute-done.refs_0_
  11.2 0.3 copy-done.1
  11.5 1.3 %shard_map.78 = (f32[8,4,2,512]{3,2,1,0:T(2,128)S(1)}, f32[8,4,2,512]{3,2,1,0:T(2,128)S(1)}, f32[2,8,2,512]{3,2,1,0:T(2,128)S(1)}) custom-call(f32[8,2,512]{2,1,0:T(2,128)S(1)} %collective-permute-done.refs_0_, f32[8,4,2,512]{3,2,1,0:T(2,128)S(1)} %shard_map.77.refs_1_, f32[8,4,2,16,512]{4,3,2,1,0:T(8,128)S(1)} %copy-done.1, f32[8,4,16]{2,1,0:T(4,128)S(1)} %copy-done.3, ...), custom_call_target="tpu_custom_call" | custom-call | tf_op jit(solution)/shard_map/pallas_call | solution.py:64
  12.9 0.1 collective-permute-start.1
  13.0 4.2 %collective-permute-done.1.refs_0_ = f32[2,8,2,512]{3,2,1,0:T(2,128)S(1)} collective-permute-done((f32[2,8,2,512]{3,2,1,0:T(2,128)S(1)}, f32[2,8,2,512]{3,2,1,0:T(2,128)S(1)}, u32[]{:S(2)}, u32[]{:S(2)}) %collective-permute-start.1) | collective-permute-done | bytes 65568 | tf_op jit(solution)/shard_map/ppermute | solution.py:84
  17.2 0.0 copy-done.4
  17.2 1.6 %shard_map.79 = (f32[8,4,2,512]{3,2,1,0:T(2,128)S(1)}, f32[8,4,2,512]{3,2,1,0:T(2,128)S(1)}, f32[32,128]{1,0:T(8,128)S(1)}) custom-call(f32[2,8,2,512]{3,2,1,0:T(2,128)S(1)} %collective-permute-done.1.refs_0_, f32[8,4,2,512]{3,2,1,0:T(2,128)S(1)} %get-tuple-element.9.refs_1_.r_ref, f32[8,4,2,512]{3,2,1,0:T(2,128)S(1)} %get-tuple-element.10.refs_2_, ...), custom_call_target="tpu_custom_call" | custom-call | tf_op jit(solution)/shard_map/pallas_call | solution.py:64
  18.8 12.0 %all_to_all.11 = f32[32,1,128]{2,1,0:T(1,128)S(1)} all-to-all(f32[32,1,128]{2,1,0:T(1,128)S(1)} %bitcast.21), channel_id=1, replica_groups=mesh['ma'=16,'freq'=2] {'ma','freq'}, dimensions={0} | all-to-all | bytes 32768 | tf_op jit(solution)/shard_map/all_to_all | solution.py:190
  30.8 0.8 %shard_map.80 = (f32[8,4,2,512]{3,2,1,0:T(2,128)}, f32[8,4,2,512]{3,2,1,0:T(2,128)}) custom-call(f32[32,128]{1,0:T(8,128)S(1)} %bitcast.14, f32[8,4,2,512]{3,2,1,0:T(2,128)S(1)} %copy-done.2, f32[8,4,2,512]{3,2,1,0:T(2,128)S(1)} %get-tuple-element.9.refs_1_.r_ref, f32[8,4,2,512]{3,2,1,0:T(2,128)S(1)} %get-tuple-element.12.w_ref, ...), custom_call_target="tpu_custom_call" | custom-call | tf_op jit(solution)/shard_map/pallas_call | solution.py:64
Async XLA Ops:
  1.4 9.8 %collective-permute-start = (f32[8,2,512]{2,1,0:T(2,128)S(1)}, f32[8,2,512]{2,1,0:T(2,128)S(1)}, u32[]{:S(2)}, u32[]{:S(2)}) collective-permute-start(f32[8,2,512]{2,1,0:T(2,128)S(1)} %fusion), channel_id=1, source_target_pairs={{0,1},{1,0},{2,3},{3,2},{4,5},{5,4},{6,7},{7,6},{8,9},{9,8},{10,11... | collective-permute-start | bytes 98312 | tf_op jit(solution)/shard_map/ppermute | solution.py:84
  4.5 1.6 %copy-start = (f32[8,4,2,16,512]{4,3,2,1,0:T(8,128)S(1)}, f32[8,4,2,16,512]{4,3,2,1,0:T(8,128)}, u32[]{:S(2)}) copy-start(f32[8,4,2,16,512]{4,3,2,1,0:T(8,128)} %refs_3_.3) | copy-start | bytes 6291460
  6.1 0.9 %copy-start.2 = (f32[8,4,2,512]{3,2,1,0:T(2,128)S(1)}, f32[8,4,2,512]{3,2,1,0:T(2,128)}, u32[]{:S(2)}) copy-start(f32[8,4,2,512]{3,2,1,0:T(2,128)} %x_ref.3) | copy-start | bytes 393220
  7.0 0.7 %copy-start.3 = (f32[8,4,16]{2,1,0:T(4,128)S(1)}, f32[8,4,16]{2,1,0:T(4,128)}, u32[]{:S(2)}) copy-start(f32[8,4,16]{2,1,0:T(4,128)} %refs_4_.1) | copy-start | bytes 6148
  7.7 0.9 %copy-start.5 = (f32[8,4,2,512]{3,2,1,0:T(2,128)S(1)}, f32[8,4,2,512]{3,2,1,0:T(2,128)}, u32[]{:S(2)}) copy-start(f32[8,4,2,512]{3,2,1,0:T(2,128)} %b_ref.1) | copy-start | bytes 393220
  8.6 0.7 %copy-start.6 = (f32[512]{0:T(512)S(1)}, f32[512]{0:T(512)}, u32[]{:S(2)}) copy-start(f32[512]{0:T(512)} %param.10) | copy-start | bytes 6148
  9.3 0.7 %copy-start.7 = (f32[512]{0:T(512)S(1)}, f32[512]{0:T(512)}, u32[]{:S(2)}) copy-start(f32[512]{0:T(512)} %param.11) | copy-start | bytes 6148
  9.9 1.6 %copy-start.1 = (f32[8,4,2,16,512]{4,3,2,1,0:T(8,128)S(1)}, f32[8,4,2,16,512]{4,3,2,1,0:T(8,128)}, u32[]{:S(2)}) copy-start(f32[8,4,2,16,512]{4,3,2,1,0:T(8,128)} %refs_3_.3) | copy-start | bytes 6291460
  10.0 7.3 %copy-start.4 = (f32[8,4,16]{2,1,0:T(4,128)S(1)}, f32[8,4,16]{2,1,0:T(4,128)}, u32[]{:S(2)}) copy-start(f32[8,4,16]{2,1,0:T(4,128)} %refs_4_.1) | copy-start | bytes 6148
  12.9 4.3 %collective-permute-start.1 = (f32[2,8,2,512]{3,2,1,0:T(2,128)S(1)}, f32[2,8,2,512]{3,2,1,0:T(2,128)S(1)}, u32[]{:S(2)}, u32[]{:S(2)}) collective-permute-start(f32[2,8,2,512]{3,2,1,0:T(2,128)S(1)} %get-tuple-element.8), channel_id=1, source_target_pairs={{0,1},{1,0},{2,3},{3,2},{4,5},{5,4},{6,7},{7,6},{8,9},{9,8},{10,11... | collective-permute-start | bytes 196616 | tf_op jit(solution)/shard_map/ppermute | solution.py:84

commit v2 on v1

v2 whole, which is shorter than its diff:
```python
import jax
import jax.numpy as jnp
from jax import lax
from jax.experimental import pallas as pl
from jax.experimental.pallas import tpu as pltpu
from jax.sharding import PartitionSpec as P

AXES = ("ma", "freq")
LANES = 128
VMEM_LIMIT = 12 * 1024 * 1024


def column(row):
    size = row.shape[1]
    spread = jnp.broadcast_to(row, (size, size))
    diagonal = lax.broadcasted_iota(jnp.int32, (size, size), 0) == lax.broadcasted_iota(
        jnp.int32, (size, size), 1
    )
    return jnp.sum(jnp.where(diagonal, spread, 0.0), axis=1, keepdims=True)


def stacked(real, imaginary):
    shape = (2, real.shape[1])
    first = lax.broadcasted_iota(jnp.int32, shape, 0) == 0
    return jnp.where(first, jnp.broadcast_to(real, shape), jnp.broadcast_to(imaginary, shape))


def beam_row(beam_ref, m, f, row, gain):
    real, imaginary = beam_ref[m, f, 0], beam_ref[m, f, 1]
    v_real, v_imag = row[0:1], row[1:2]
    p_real = jnp.sum(real * v_real + imaginary * v_imag, axis=1, keepdims=True) * gain
    p_imag = jnp.sum(real * v_imag - imaginary * v_real, axis=1, keepdims=True) * gain
    back_real = jnp.sum(real * p_real - imaginary * p_imag, axis=0, keepdims=True)
    back_imag = jnp.sum(real * p_imag + imaginary * p_real, axis=0, keepdims=True)
    return stacked(back_real, back_imag)


def counts(index, size, length):
    total = size * length
    out = []
    for f in range(length):
        channel = index * length + f
        out.append(
            jnp.where(channel > 0, 1.0, 0.0) + jnp.where(channel < total - 1, 1.0, 0.0)
        )
    return out


def local_rows(rows, m, beam_ref, noise_ref, inv, smooth, weights):
    out = []
    gains = noise_ref[m]
    for f, row in enumerate(rows):
        prior = weights[f] * row
        if f > 0:
            prior = prior - rows[f - 1]
        if f + 1 < len(rows):
            prior = prior - rows[f + 1]
        image = beam_row(beam_ref, m, f, row, column(gains[f : f + 1]))
        out.append(image + inv * row + smooth * prior)
    return out


def call(body, outs, *args, **options):
    return pl.pallas_call(
        body,
        out_shape=outs,
        compiler_params=pltpu.CompilerParams(vmem_limit_bytes=VMEM_LIMIT),
        **options,
    )(*args)


def shards(size, devices, right_side, start_field, beam, noise, inv_power, smooth):
    modes, length = right_side.shape[:2]
    width = right_side.shape[3]
    assert length > 2
    pair = size == 2
    ways = 1 if pair else 2
    field = jax.ShapeDtypeStruct(right_side.shape, jnp.float32)
    edge = jax.ShapeDtypeStruct((modes, 2, width), jnp.float32)
    edge_pair = jax.ShapeDtypeStruct((2, modes, 2, width), jnp.float32)
    inv_power = inv_power.reshape(1, width)
    smooth = smooth.reshape(1, width)
    up = [(i, i + 1) for i in range(size - 1)]
    down = [(j, i) for i, j in up]

    def exchanged(sends):
        if pair:
            return [lax.ppermute(sends[0], "freq", up + down)]
        return [lax.ppermute(sends[1], "freq", up), lax.ppermute(sends[0], "freq", down)]

    def place():
        at = lax.axis_index("freq")
        below, above = at > 0, at < size - 1
        rows = [jnp.where(at == 0, length - 1, 0)] if pair else [0, length - 1]
        exists = [True] if pair else [below, above]
        return at, below, above, rows, exists

    def first(x_hbm, b_hbm, beam_hbm, noise_hbm, inv_hbm, smooth_hbm, p_ref, *refs):
        send_refs, refs = refs[:ways], refs[ways:]
        x_ref, b_ref, beam_ref, noise_ref, inv_ref, smooth_ref, few, many = refs
        small = [
            pltpu.make_async_copy(source, target, few.at[i])
            for i, (source, target) in enumerate(
                (
                    (x_hbm, x_ref),
                    (noise_hbm, noise_ref),
                    (inv_hbm, inv_ref),
                    (smooth_hbm, smooth_ref),
                    (b_hbm, b_ref),
                )
            )
        ]

        def large(m):
            return pltpu.make_async_copy(beam_hbm.at[m], beam_ref.at[m], many.at[m])

        for copy in small:
            copy.start()
        for m in range(modes):
            large(m).start()
        for copy in small:
            copy.wait()
        at, _, _, ends, _ = place()
        inv, strength = inv_ref[...], smooth_ref[...]
        weights = counts(at, size, length)

        def step(m, _):
            large(m).wait()
            rows = [x_ref[m, f] for f in range(length)]
            images = local_rows(rows, m, beam_ref, noise_ref, inv, strength, weights)
            for f in range(length):
                p_ref[m, f] = b_ref[m, f] - images[f]
            for ref, end in zip(send_refs, ends):
                ref[0, m] = x_ref[m, end]
                ref[1, m] = p_ref[m, end]
            return 0

        lax.fori_loop(0, modes, step, 0)

    loads = (start_field, right_side, beam, noise, inv_power, smooth)
    partial, *sends = call(
        first,
        (field,) + (edge_pair,) * ways,
        *[pltpu.with_memory_space_constraint(array, pltpu.HBM) for array in loads],
        in_specs=[pl.BlockSpec(memory_space=pltpu.HBM)] * len(loads),
        scratch_shapes=[pltpu.VMEM(array.shape, jnp.float32) for array in loads]
        + [pltpu.SemaphoreType.DMA((len(loads) - 1,)), pltpu.SemaphoreType.DMA((modes,))],
    )
    halos = exchanged(sends)

    def second(p_ref, beam_ref, noise_ref, inv_ref, smooth_ref, y_ref):
        at = lax.axis_index("freq")
        inv, strength = inv_ref[...], smooth_ref[...]
        weights = counts(at, size, length)

        def step(m, _):
            rows = [p_ref[m, f] for f in range(length)]
            images = local_rows(rows, m, beam_ref, noise_ref, inv, strength, weights)
            for f in range(length):
                y_ref[m, f] = images[f]
            return 0

        lax.fori_loop(0, modes, step, 0)

    image = call(second, field, partial, beam, noise, inv_power, smooth)

    def correct(*refs):
        halo_refs, send_refs, refs = refs[:ways], refs[ways : 2 * ways], refs[2 * ways :]
        p_ref, y_ref, beam_ref, noise_ref, inv_ref, smooth_ref = refs[:6]
        out_refs = refs[6:]
        at, _, _, ends, exists = place()
        inv, strength = inv_ref[...], smooth_ref[...]
        total = size * length

        def step(m, _):
            for halo, send, out, end, there in zip(halo_refs, send_refs, out_refs, ends, exists):
                channel = at * length + end
                weight = jnp.where(channel > 0, 1.0, 0.0) + jnp.where(channel < total - 1, 1.0, 0.0)
                added = strength * halo[0, m]
                theirs = halo[1, m] + strength * send[0, m]
                gain = column(noise_ref[m, pl.ds(end, 1), :])
                image = beam_row(beam_ref, m, end, added, gain)
                change = image + (inv + strength * weight) * added - strength * theirs
                out[m] = y_ref[m, end] + (change if there is True else jnp.where(there, change, 0.0))
            return 0

        lax.fori_loop(0, modes, step, 0)

    along_ends = call(
        correct, (edge,) * ways, *halos, *sends, partial, image, beam, noise, inv_power, smooth
    )
    far_ends = exchanged(along_ends)

    def third(*refs):
        halo_refs, end_refs, refs = refs[:ways], refs[ways : 2 * ways], refs[2 * ways :]
        p_ref, y_ref, beam_ref, noise_ref, inv_ref, smooth_ref = refs[:6]
        r_ref, w_ref, z_ref, sums_ref = refs[6:]
        at, below, above, _, _ = place()
        inv, strength = inv_ref[...], smooth_ref[...]
        weights = counts(at, size, length)

        def step(m, sums):
            added_low = jnp.where(below, strength * halo_refs[0][0, m], 0.0)
            added_high = jnp.where(above, strength * halo_refs[-1][0, m], 0.0)
            resids = [p_ref[m, f] for f in range(length)]
            resids[0] = resids[0] + added_low
            resids[-1] = resids[-1] + added_high
            rows = [y_ref[m, f] for f in range(length)]
            rows[0] = jnp.where(below, end_refs[0][m], rows[0])
            rows[-1] = jnp.where(above, end_refs[-1][m], rows[-1])
            rows[1] = rows[1] - strength * added_low
            rows[-2] = rows[-2] - strength * added_high
            images = local_rows(rows, m, beam_ref, noise_ref, inv, strength, weights)
            rr, rw, ww, wz = sums
            for f in range(length):
                r_ref[m, f] = resids[f]
                w_ref[m, f] = rows[f]
                z_ref[m, f] = images[f]
                rr = rr + resids[f] * resids[f]
                rw = rw + resids[f] * rows[f]
                ww = ww + rows[f] * rows[f]
                wz = wz + rows[f] * images[f]
            return rr, rw, ww, wz

        zero = jnp.zeros((2, width), jnp.float32)
        sums = lax.fori_loop(0, modes, step, (zero, zero, zero, zero))
        lane = lax.broadcasted_iota(jnp.int32, (1, LANES), 1)
        packed = jnp.zeros((1, LANES), jnp.float32)
        for at_lane, value in enumerate(sums):
            packed = jnp.where(lane == at_lane, jnp.sum(value), packed)
        sums_ref[...] = packed

    resid, along, twice, sums = call(
        third,
        (field, field, field, jax.ShapeDtypeStruct((1, LANES), jnp.float32)),
        *halos, *along_ends, partial, image, beam, noise, inv_power, smooth,
    )

    def cross(*refs):
        far_refs, end_refs, (sums_ref, smooth_ref, out_ref) = refs[:ways], refs[ways:-3], refs[-3:]
        _, _, _, _, exists = place()
        strength = smooth_ref[...]
        total = jnp.zeros((1, 1), jnp.float32)
        for far, end, there in zip(far_refs, end_refs, exists):
            product = jnp.sum(far[...] * end[...], axis=0)
            value = jnp.sum(strength * product, keepdims=True)
            total = total + (value if there is True else jnp.where(there, value, 0.0))
        lane = lax.broadcasted_iota(jnp.int32, (1, LANES), 1)
        packed = sums_ref[...] - jnp.where(lane == 3, total, 0.0)
        out_ref[...] = jnp.broadcast_to(packed, (devices, LANES))

    sums = call(
        cross, jax.ShapeDtypeStruct((devices, LANES), jnp.float32), *far_ends, *along_ends, sums, smooth
    )
    sums = lax.all_to_all(sums, AXES, 0, 0, tiled=True)

    def last(*refs):
        far_refs, refs = refs[:ways], refs[ways:]
        sums_ref, x_ref, r_ref, w_ref, z_ref, smooth_ref, out_ref, resid_ref = refs
        _, _, _, ends, exists = place()
        total = jnp.sum(sums_ref[...], axis=0, keepdims=True)
        lane = lax.broadcasted_iota(jnp.int32, (1, LANES), 1)
        rr, rw, ww, wz = [
            jnp.sum(jnp.where(lane == i, total, 0.0), axis=1, keepdims=True) for i in range(4)
        ]
        step0 = rr / rw
        crossed = rw - step0 * ww
        rr1 = rr - 2.0 * step0 * rw + step0 * step0 * ww
        growth = rr1 / rr
        curve = rw - 2.0 * step0 * ww + step0 * step0 * wz + growth * crossed
        step1 = rr1 / curve
        on_r = (step0 + step1 * (1.0 + growth)).reshape(1, 1, 1, 1)
        on_w = (step1 * step0).reshape(1, 1, 1, 1)
        r, w = r_ref[...], w_ref[...]
        out_ref[...] = x_ref[...] + on_r * r - on_w * w
        resid_ref[...] = r - on_r * w + on_w * z_ref[...]
        scale = (step1 * step0).reshape(1, 1, 1) * smooth_ref[...].reshape(1, 1, width)
        for far, end, there in zip(far_refs, ends, exists):
            value = scale * far[...]
            value = value if there is True else jnp.where(there, value, 0.0)
            resid_ref[:, end] = resid_ref[:, end] - value

    return tuple(
        call(last, (field, field), *far_ends, sums, start_field, resid, along, twice, smooth)
    )


def solution(mesh):
    size, devices = mesh.shape["freq"], mesh.size

    def body(*args):
        return shards(size, devices, *args)

    in_specs = (
        P("ma", "freq", None, None),
        P("ma", "freq", None, None),
        P("ma", "freq", None, None, None),
        P("ma", "freq", None),
        P(),
        P(),
    )
    out_specs = (P("ma", "freq", None, None), P("ma", "freq", None, None))
    return jax.shard_map(body, mesh=mesh, in_specs=in_specs, out_specs=out_specs, check_vma=False)
```

time: 32 us -> 28.5 us (0.89)
  local copies, waits for them, and re-layouts: 5.77 us -> 0.02 us
  waiting for transfers between devices: 4.25 us -> 1.21 us
  Pallas kernels: 5.03 us -> 7.9 us
  starting transfers between devices: 3.11 us -> 5.08 us
  blocking collectives: 12 us -> 13.4 us
  other arithmetic: 0.8 us -> 0 us
    unnamed x16 -> x10, local copies, waits for them, and re-layouts: 5.77 us -> 0.02 us
    ppermute x2, waiting for transfers between devices: 4.25 us -> 1.21 us  [exchanged(): return [lax.ppermute(sends[0], 'freq', up + down)]]
    pallas_call x4 -> x6, Pallas kernels: 5.03 us -> 7.9 us  [call(): pl.pallas_call(body, out_shape=outs, compiler_params=pltpu.CompilerParams...]
    ppermute x2, starting transfers between devices: 3.11 us -> 5.08 us  [exchanged(): return [lax.ppermute(sends[0], 'freq', up + down)]]
    all_to_all x1, blocking collectives: 12 us -> 13.4 us  [shards(): sums = lax.all_to_all(sums, AXES, 0, 0, tiled=True)]
    select_n x1 -> x0, other arithmetic: 0.8 us -> none  [edges(): return [jnp.where(at == 0, last, first)] if pair else [last, first]]
  transfers between devices with their start and end apart: 2 -> 2, of which waited for: 1 -> 2; matrix products, arithmetic and copies ran while one was open for 0% -> 0% of each run, Pallas kernels for 4% -> 10%
where the time goes in v2:
time: 28.5 us; the launch traced here: 28.3 us
  blocking collectives  13.4 us (47%)
  Pallas kernels  7.9 us (28%)
  starting transfers between devices  5.08 us (18%)
  waiting for transfers between devices  1.21 us (4%)
  between operations  0.72 us (3%)
    all_to_all x1, blocking collectives, shards(): sums = lax.all_to_all(sums, AXES, 0, 0, tiled=True)  13.4 us
    pallas_call x6, Pallas kernels, call(): pl.pallas_call(body, out_shape=outs, compiler_params=pltpu.CompilerParams...  7.9 us
    ppermute x2, starting transfers between devices, exchanged(): return [lax.ppermute(sends[0], 'freq', up + down)]  5.08 us
    ppermute x2, waiting for transfers between devices, exchanged(): return [lax.ppermute(sends[0], 'freq', up + down)]  1.21 us
  transfers between devices with their start and end apart: 2, of which 2 were waited for; matrix products, arithmetic and copies ran while one was open for 0% of the time, Pallas kernels for 10%

profile of v2, /device:TPU:0, one launch (start us, length us, event | category | flops | bytes accessed | tf_op | source)
XLA Modules:
  0.0 28.3 jit_solution(12053736498950918438)
XLA Ops:
  0.6 0.0 copy-start.3
  0.6 0.0 copy-start.4
  0.7 0.0 copy-start
  0.7 0.0 copy-start.2
  0.7 3.1 %shard_map.77 = (f32[8,4,2,512]{3,2,1,0:T(2,128)S(1)}, f32[2,8,2,512]{3,2,1,0:T(2,128)S(1)}) custom-call(f32[8,4,2,512]{3,2,1,0:T(2,128)} %refs_2_.1, f32[8,4,2,512]{3,2,1,0:T(2,128)} %b_hbm.1, f32[8,4,2,16,512]{4,3,2,1,0:T(8,128)} %refs_4_.3, f32[8,4,16]{2,1,0:T(4,128)} %refs_5_.3, f32[1,512]{1,0:T(1,128)} %bitcast.14, f32[1,512]{1,0:T(1,128)} %bitcast.6), custom_call_target="tpu_custom_call" | custom-call | tf_op jit(solution)/shard_map/pallas_call | solution.py:64
  3.8 3.0 %collective-permute-start = (f32[2,8,2,512]{3,2,1,0:T(2,128)S(1)}, f32[2,8,2,512]{3,2,1,0:T(2,128)S(1)}, u32[]{:S(2)}, u32[]{:S(2)}) collective-permute-start(f32[2,8,2,512]{3,2,1,0:T(2,128)S(1)} %get-tuple-element.8.refs_1_), channel_id=1, source_target_pairs={{0,1},{1,0},{2,3},{3,2},{4,5},{5,4},{6,7},{7,6},{8,9},{9,8},{10,11... | collective-permute-start | bytes 196616 | tf_op jit(solution)/shard_map/ppermute | solution.py:88
  6.8 0.0 copy-done.3
  6.8 0.0 copy-done.4
  6.8 0.0 copy-done
  6.8 0.0 copy-done.2
  6.8 1.3 %shard_map.78.refs_3_ = f32[8,4,2,512]{3,2,1,0:T(2,128)S(1)} custom-call(f32[8,4,2,512]{3,2,1,0:T(2,128)S(1)} %get-tuple-element.9.p_ref.refs_2_, f32[8,4,2,16,512]{4,3,2,1,0:T(8,128)S(1)} %copy-done, f32[8,4,16]{2,1,0:T(4,128)S(1)} %copy-done.2, f32[1,512]{1,0:T(1,128)S(1)} %bitcast.15, f32[1,512]{1,0:T(1,128)S(1)} %bitcast.7), custom_call_target="tpu_custom_call" | custom-call | tf_op jit(solution)/shard_map/pallas_call | solution.py:64
  8.1 0.0 copy-start.1
  8.1 0.9 %collective-permute-done.refs_0_ = f32[2,8,2,512]{3,2,1,0:T(2,128)S(1)} collective-permute-done((f32[2,8,2,512]{3,2,1,0:T(2,128)S(1)}, f32[2,8,2,512]{3,2,1,0:T(2,128)S(1)}, u32[]{:S(2)}, u32[]{:S(2)}) %collective-permute-start) | collective-permute-done | bytes 65568 | tf_op jit(solution)/shard_map/ppermute | solution.py:88
  9.0 0.9 %shard_map.79.refs_1_ = f32[8,2,512]{2,1,0:T(2,128)S(1)} custom-call(f32[2,8,2,512]{3,2,1,0:T(2,128)S(1)} %collective-permute-done.refs_0_, f32[2,8,2,512]{3,2,1,0:T(2,128)S(1)} %get-tuple-element.8.refs_1_, f32[8,4,2,512]{3,2,1,0:T(2,128)S(1)} %get-tuple-element.9.p_ref.refs_2_, f32[8,4,2,512]{3,2,1,0:T(2,128)S(1)} %shard_map.78.refs_3_, ...), custom_call_target="tpu_custom_call" | custom-call | tf_op jit(solution)/shard_map/pallas_call | solution.py:64
  10.0 2.1 %collective-permute-start.1 = (f32[8,2,512]{2,1,0:T(2,128)S(1)}, f32[8,2,512]{2,1,0:T(2,128)S(1)}, u32[]{:S(2)}, u32[]{:S(2)}) collective-permute-start(f32[8,2,512]{2,1,0:T(2,128)S(1)} %shard_map.79.refs_1_), channel_id=1, source_target_pairs={{0,1},{1,0},{2,3},{3,2},{4,5},{5,4},{6,7},{7,6},{8,9},{9,8},{10,11... | collective-permute-start | bytes 98312 | tf_op jit(solution)/shard_map/ppermute | solution.py:88
  12.0 1.6 %shard_map.80 = (f32[8,4,2,512]{3,2,1,0:T(2,128)S(1)}, f32[8,4,2,512]{3,2,1,0:T(2,128)S(1)}, f32[8,4,2,512]{3,2,1,0:T(2,128)S(1)}, f32[1,128]{1,0:T(1,128)S(1)}) custom-call(f32[2,8,2,512]{3,2,1,0:T(2,128)S(1)} %collective-permute-done.refs_0_, f32[8,2,512]{2,1,0:T(2,128)S(1)} %shard_map.79.refs_1_, f32[8,4,2,512]{3,2,1,0:T(2,128)S(1)} %get-tuple-element.9.p_ref.refs_2_, ...), custom_call_target="tpu_custom_call" | custom-call | tf_op jit(solution)/shard_map/pallas_call | solution.py:64
  13.6 0.3 %collective-permute-done.1.refs_0_ = f32[8,2,512]{2,1,0:T(2,128)S(1)} collective-permute-done((f32[8,2,512]{2,1,0:T(2,128)S(1)}, f32[8,2,512]{2,1,0:T(2,128)S(1)}, u32[]{:S(2)}, u32[]{:S(2)}) %collective-permute-start.1) | collective-permute-done | bytes 32800 | tf_op jit(solution)/shard_map/ppermute | solution.py:88
  13.9 0.1 shard_map.81
  14.1 13.4 %all_to_all.11 = f32[32,1,128]{2,1,0:T(1,128)S(1)} all-to-all(f32[32,1,128]{2,1,0:T(1,128)S(1)} %bitcast.13), channel_id=1, replica_groups=mesh['ma'=16,'freq'=2] {'ma','freq'}, dimensions={0} | all-to-all | bytes 32768 | tf_op jit(solution)/shard_map/all_to_all | solution.py:255
  27.5 0.0 copy-done.1
  27.5 0.8 %shard_map.82 = (f32[8,4,2,512]{3,2,1,0:T(2,128)}, f32[8,4,2,512]{3,2,1,0:T(2,128)}) custom-call(f32[8,2,512]{2,1,0:T(2,128)S(1)} %collective-permute-done.1.refs_0_, f32[32,128]{1,0:T(8,128)S(1)} %bitcast.12, f32[8,4,2,512]{3,2,1,0:T(2,128)S(1)} %copy-done.1, f32[8,4,2,512]{3,2,1,0:T(2,128)S(1)} %get-tuple-element.11.refs_3_, ...), custom_call_target="tpu_custom_call" | custom-call | tf_op jit(solution)/shard_map/pallas_call | solution.py:64
Async XLA Ops:
  0.6 6.2 %copy-start.3 = (f32[512]{0:T(512)S(1)}, f32[512]{0:T(512)}, u32[]{:S(2)}) copy-start(f32[512]{0:T(512)} %param.11) | copy-start | bytes 6148
  0.6 6.2 %copy-start.4 = (f32[512]{0:T(512)S(1)}, f32[512]{0:T(512)}, u32[]{:S(2)}) copy-start(f32[512]{0:T(512)} %param.10) | copy-start | bytes 6148
  0.7 6.1 %copy-start = (f32[8,4,2,16,512]{4,3,2,1,0:T(8,128)S(1)}, f32[8,4,2,16,512]{4,3,2,1,0:T(8,128)}, u32[]{:S(2)}) copy-start(f32[8,4,2,16,512]{4,3,2,1,0:T(8,128)} %refs_4_.3) | copy-start | bytes 6291460
  0.7 6.1 %copy-start.2 = (f32[8,4,16]{2,1,0:T(4,128)S(1)}, f32[8,4,16]{2,1,0:T(4,128)}, u32[]{:S(2)}) copy-start(f32[8,4,16]{2,1,0:T(4,128)} %refs_5_.3) | copy-start | bytes 6148
  3.8 5.2 %collective-permute-start = (f32[2,8,2,512]{3,2,1,0:T(2,128)S(1)}, f32[2,8,2,512]{3,2,1,0:T(2,128)S(1)}, u32[]{:S(2)}, u32[]{:S(2)}) collective-permute-start(f32[2,8,2,512]{3,2,1,0:T(2,128)S(1)} %get-tuple-element.8.refs_1_), channel_id=1, source_target_pairs={{0,1},{1,0},{2,3},{3,2},{4,5},{5,4},{6,7},{7,6},{8,9},{9,8},{10,11... | collective-permute-start | bytes 196616 | tf_op jit(solution)/shard_map/ppermute | solution.py:88
  8.1 19.4 %copy-start.1 = (f32[8,4,2,512]{3,2,1,0:T(2,128)S(1)}, f32[8,4,2,512]{3,2,1,0:T(2,128)}, u32[]{:S(2)}) copy-start(f32[8,4,2,512]{3,2,1,0:T(2,128)} %refs_2_.1) | copy-start | bytes 393220
  10.0 4.0 %collective-permute-start.1 = (f32[8,2,512]{2,1,0:T(2,128)S(1)}, f32[8,2,512]{2,1,0:T(2,128)S(1)}, u32[]{:S(2)}, u32[]{:S(2)}) collective-permute-start(f32[8,2,512]{2,1,0:T(2,128)S(1)} %shard_map.79.refs_1_), channel_id=1, source_target_pairs={{0,1},{1,0},{2,3},{3,2},{4,5},{5,4},{6,7},{7,6},{8,9},{9,8},{10,11... | collective-permute-start | bytes 98312 | tf_op jit(solution)/shard_map/ppermute | solution.py:88

commit v3 on v2

v3 whole, which is shorter than its diff:
```python
import jax
import jax.numpy as jnp
from jax import lax
from jax.experimental import pallas as pl
from jax.experimental.pallas import tpu as pltpu
from jax.sharding import PartitionSpec as P

AXES = ("ma", "freq")
LANES = 128
VMEM_LIMIT = 12 * 1024 * 1024


def column(row):
    size = row.shape[1]
    spread = jnp.broadcast_to(row, (size, size))
    diagonal = lax.broadcasted_iota(jnp.int32, (size, size), 0) == lax.broadcasted_iota(
        jnp.int32, (size, size), 1
    )
    return jnp.sum(jnp.where(diagonal, spread, 0.0), axis=1, keepdims=True)


def stacked(real, imaginary):
    shape = (2, real.shape[1])
    first = lax.broadcasted_iota(jnp.int32, shape, 0) == 0
    return jnp.where(first, jnp.broadcast_to(real, shape), jnp.broadcast_to(imaginary, shape))


def beam_row(real, imaginary, row, gain):
    v_real, v_imag = row[0:1], row[1:2]
    p_real = jnp.sum(real * v_real + imaginary * v_imag, axis=1, keepdims=True) * gain
    p_imag = jnp.sum(real * v_imag - imaginary * v_real, axis=1, keepdims=True) * gain
    back_real = jnp.sum(real * p_real - imaginary * p_imag, axis=0, keepdims=True)
    back_imag = jnp.sum(real * p_imag + imaginary * p_real, axis=0, keepdims=True)
    return stacked(back_real, back_imag)


def call(body, outs, *args, **options):
    return pl.pallas_call(
        body,
        out_shape=outs,
        compiler_params=pltpu.CompilerParams(vmem_limit_bytes=VMEM_LIMIT),
        **options,
    )(*args)


def shards(size, devices, right_side, start_field, beam, noise, inv_power, smooth):
    modes, length, _, width = right_side.shape
    assert length > 2
    pair = size == 2
    ways = 1 if pair else 2
    ends = [0] if pair else [0, length - 1]
    inner = [j for j in range(length) if j not in ends]
    field = jax.ShapeDtypeStruct(right_side.shape, jnp.float32)
    edge = jax.ShapeDtypeStruct((modes, 2, width), jnp.float32)
    edge_pair = jax.ShapeDtypeStruct((2, modes, 2, width), jnp.float32)
    inv_power = inv_power.reshape(1, width)
    smooth = smooth.reshape(1, width)
    up = [(i, i + 1) for i in range(size - 1)]
    down = [(j, i) for i, j in up]

    def exchanged(sends):
        if pair:
            return [lax.ppermute(sends[0], "freq", up + down)]
        return [lax.ppermute(sends[1], "freq", up), lax.ppermute(sends[0], "freq", down)]

    def place():
        at = lax.axis_index("freq")
        if pair:
            order = [jnp.where(at == 0, length - 1 - j, j) for j in range(length)]
        else:
            order = list(range(length))
        weights = []
        for f in order:
            channel = at * length + f
            weights.append(
                jnp.where(channel > 0, 1.0, 0.0)
                + jnp.where(channel < size * length - 1, 1.0, 0.0)
            )
        exists = [True] if pair else [at > 0, at < size - 1]
        return order, weights, exists

    def kept(there, value):
        return value if there is True else jnp.where(there, value, 0.0)

    def operator(beam_of, noise_of, inv, strength, weights):
        def apply(rows, j):
            prior = weights[j] * rows[j]
            if j > 0:
                prior = prior - rows[j - 1]
            if j + 1 < length:
                prior = prior - rows[j + 1]
            real, imaginary = beam_of(j)
            image = beam_row(real, imaginary, rows[j], column(noise_of(j)))
            return image + inv * rows[j] + strength * prior

        return apply

    def whole(m, order, beam_ref, noise_ref, inv, strength, weights):
        return operator(
            lambda j: (beam_ref[m, order[j], 0], beam_ref[m, order[j], 1]),
            lambda j: noise_ref[m, pl.ds(order[j], 1), :],
            inv, strength, weights,
        )

    def first(x_hbm, b_hbm, beam_hbm, noise_hbm, inv_hbm, smooth_hbm, *refs):
        send_refs, refs = refs[:ways], refs[ways:]
        x_ref, b_ref, beam_ref, noise_ref, inv_ref, smooth_ref, sems = refs
        order, weights, _ = place()
        copies = [(beam_hbm.at[:, order[j]], beam_ref.at[k]) for k, j in enumerate(ends)]
        copies += [(b_hbm.at[:, order[j]], b_ref.at[k]) for k, j in enumerate(ends)]
        copies += [
            (x_hbm, x_ref), (noise_hbm, noise_ref), (inv_hbm, inv_ref), (smooth_hbm, smooth_ref)
        ]
        copies = [
            pltpu.make_async_copy(source, target, sems.at[i])
            for i, (source, target) in enumerate(copies)
        ]
        for copy in copies:
            copy.start()
        for copy in copies:
            copy.wait()
        inv, strength = inv_ref[...], smooth_ref[...]

        def step(m, _):
            rows = [x_ref[m, f] for f in order]
            for k, j in enumerate(ends):
                apply = operator(
                    lambda j, k=k: (beam_ref[k, m, 0], beam_ref[k, m, 1]),
                    lambda j: noise_ref[m, pl.ds(order[j], 1), :],
                    inv, strength, weights,
                )
                send_refs[k][0, m] = rows[j]
                send_refs[k][1, m] = b_ref[k, m] - apply(rows, j)
            return 0

        lax.fori_loop(0, modes, step, 0, unroll=True)

    loads = (start_field, right_side, beam, noise, inv_power, smooth)
    scratch = [
        start_field.shape,
        (ways, modes, 2, width),
        (ways, modes) + beam.shape[2:],
        noise.shape,
        (1, width),
        (1, width),
    ]
    sends = call(
        first,
        (edge_pair,) * ways,
        *[pltpu.with_memory_space_constraint(array, pltpu.HBM) for array in loads],
        in_specs=[pl.BlockSpec(memory_space=pltpu.HBM)] * len(loads),
        scratch_shapes=[pltpu.VMEM(shape, jnp.float32) for shape in scratch]
        + [pltpu.SemaphoreType.DMA((2 * ways + 4,))],
    )
    sends = list(sends)
    halos = exchanged(sends)

    def middle(x_ref, b_ref, beam_ref, noise_ref, inv_ref, smooth_ref, p_ref):
        order, weights, _ = place()
        inv, strength = inv_ref[...], smooth_ref[...]

        def step(m, _):
            apply = whole(m, order, beam_ref, noise_ref, inv, strength, weights)
            rows = [x_ref[m, f] for f in order]
            for j in inner:
                p_ref[m, j] = b_ref[m, order[j]] - apply(rows, j)
            return 0

        lax.fori_loop(0, modes, step, 0, unroll=2)

    partial = call(middle, field, start_field, right_side, beam, noise, inv_power, smooth)

    def second(*refs):
        halo_refs, send_refs, refs = refs[:ways], refs[ways : 2 * ways], refs[2 * ways :]
        p_ref, beam_ref, noise_ref, inv_ref, smooth_ref = refs[:5]
        r_refs, w_refs = refs[5 : 5 + ways], refs[5 + ways :]
        order, weights, exists = place()
        inv, strength = inv_ref[...], smooth_ref[...]

        def step(m, _):
            apply = whole(m, order, beam_ref, noise_ref, inv, strength, weights)
            rows = [None if j in ends else p_ref[m, j] for j in range(length)]
            for k, j in enumerate(ends):
                rows[j] = send_refs[k][1, m] + kept(exists[k], strength * halo_refs[k][0, m])
            for k, j in enumerate(ends):
                theirs = halo_refs[k][1, m] + strength * send_refs[k][0, m]
                r_refs[k][m] = rows[j]
                w_refs[k][m] = apply(rows, j) - kept(exists[k], strength * theirs)
            return 0

        lax.fori_loop(0, modes, step, 0, unroll=True)

    edges = call(
        second, (edge,) * (2 * ways), *halos, *sends, partial, beam, noise, inv_power, smooth
    )
    resid_ends, along_ends = edges[:ways], edges[ways:]
    far_ends = exchanged(along_ends)

    def third(*refs):
        r_ends, w_ends, refs = refs[:ways], refs[ways : 2 * ways], refs[2 * ways :]
        p_ref, beam_ref, noise_ref, inv_ref, smooth_ref = refs[:5]
        r_ref, w_ref, z_ref, sums_ref = refs[5:]
        order, weights, _ = place()
        inv, strength = inv_ref[...], smooth_ref[...]

        def step(m, sums):
            apply = whole(m, order, beam_ref, noise_ref, inv, strength, weights)
            resids = [
                r_ends[ends.index(j)][m] if j in ends else p_ref[m, j] for j in range(length)
            ]
            rows = [
                w_ends[ends.index(j)][m] if j in ends else apply(resids, j) for j in range(length)
            ]
            rr, rw, ww, wz = sums
            for j in range(length):
                image = apply(rows, j)
                r_ref[m, order[j]] = resids[j]
                w_ref[m, order[j]] = rows[j]
                z_ref[m, order[j]] = image
                rr = rr + resids[j] * resids[j]
                rw = rw + resids[j] * rows[j]
                ww = ww + rows[j] * rows[j]
                wz = wz + rows[j] * image
            return rr, rw, ww, wz

        zero = jnp.zeros((2, width), jnp.float32)
        sums = lax.fori_loop(0, modes, step, (zero, zero, zero, zero), unroll=2)
        lane = lax.broadcasted_iota(jnp.int32, (1, LANES), 1)
        packed = jnp.zeros((1, LANES), jnp.float32)
        for at_lane, value in enumerate(sums):
            packed = jnp.where(lane == at_lane, jnp.sum(value), packed)
        sums_ref[...] = packed

    resid, along, twice, sums = call(
        third,
        (field, field, field, jax.ShapeDtypeStruct((1, LANES), jnp.float32)),
        *resid_ends, *along_ends, partial, beam, noise, inv_power, smooth,
    )

    def cross(*refs):
        far_refs, end_refs, (sums_ref, smooth_ref, out_ref) = refs[:ways], refs[ways:-3], refs[-3:]
        _, _, exists = place()
        strength = smooth_ref[...]
        total = jnp.zeros((1, 1), jnp.float32)
        for far, end, there in zip(far_refs, end_refs, exists):
            product = jnp.sum(far[...] * end[...], axis=0)
            value = jnp.sum(strength * product, keepdims=True)
            total = total + kept(there, value)
        lane = lax.broadcasted_iota(jnp.int32, (1, LANES), 1)
        packed = sums_ref[...] - jnp.where(lane == 3, total, 0.0)
        out_ref[...] = jnp.broadcast_to(packed, (devices, LANES))

    sums = call(
        cross, jax.ShapeDtypeStruct((devices, LANES), jnp.float32), *far_ends, *along_ends, sums, smooth
    )
    sums = lax.all_to_all(sums, AXES, 0, 0, tiled=True)

    def last(*refs):
        far_refs, refs = refs[:ways], refs[ways:]
        sums_ref, x_ref, r_ref, w_ref, z_ref, smooth_ref, out_ref, resid_ref = refs
        order, _, exists = place()
        total = jnp.sum(sums_ref[...], axis=0, keepdims=True)
        lane = lax.broadcasted_iota(jnp.int32, (1, LANES), 1)
        rr, rw, ww, wz = [
            jnp.sum(jnp.where(lane == i, total, 0.0), axis=1, keepdims=True) for i in range(4)
        ]
        step0 = rr / rw
        crossed = rw - step0 * ww
        rr1 = rr - 2.0 * step0 * rw + step0 * step0 * ww
        growth = rr1 / rr
        curve = rw - 2.0 * step0 * ww + step0 * step0 * wz + growth * crossed
        step1 = rr1 / curve
        on_r = (step0 + step1 * (1.0 + growth)).reshape(1, 1, 1, 1)
        on_w = (step1 * step0).reshape(1, 1, 1, 1)
        r, w = r_ref[...], w_ref[...]
        out_ref[...] = x_ref[...] + on_r * r - on_w * w
        resid_ref[...] = r - on_r * w + on_w * z_ref[...]
        scale = (step1 * step0).reshape(1, 1, 1) * smooth_ref[...].reshape(1, 1, width)
        for far, j, there in zip(far_refs, ends, exists):
            value = kept(there, scale * far[...])
            resid_ref[:, order[j]] = resid_ref[:, order[j]] - value

    return tuple(
        call(last, (field, field), *far_ends, sums, start_field, resid, along, twice, smooth)
    )


def solution(mesh):
    size, devices = mesh.shape["freq"], mesh.size

    def body(*args):
        return shards(size, devices, *args)

    in_specs = (
        P("ma", "freq", None, None),
        P("ma", "freq", None, None),
        P("ma", "freq", None, None, None),
        P("ma", "freq", None),
        P(),
        P(),
    )
    out_specs = (P("ma", "freq", None, None), P("ma", "freq", None, None))
    return jax.shard_map(body, mesh=mesh, in_specs=in_specs, out_specs=out_specs, check_vma=False)
```

time: 28.5 us -> 26.3 us (0.923)
  Pallas kernels: 7.9 us -> 5.58 us
    pallas_call x6, Pallas kernels: 7.9 us -> 5.58 us  [call(): pl.pallas_call(body, out_shape=outs, compiler_params=pltpu.CompilerParams...]
  transfers between devices with their start and end apart: 2 -> 2, of which waited for: 2 -> 1; matrix products, arithmetic and copies ran while one was open for 0% -> 0% of each run, Pallas kernels for 10% -> 11%
where the time goes in v3:
time: 26.3 us; the launch traced here: 26.2 us
  blocking collectives  13.4 us (51%)
  Pallas kernels  5.58 us (21%)
  starting transfers between devices  5.11 us (19%)
  waiting for transfers between devices  1.36 us (5%)
  between operations  0.74 us (3%)
    all_to_all x1, blocking collectives, shards(): sums = lax.all_to_all(sums, AXES, 0, 0, tiled=True)  13.4 us
    pallas_call x6, Pallas kernels, call(): pl.pallas_call(body, out_shape=outs, compiler_params=pltpu.CompilerParams...  5.58 us
    ppermute x2, starting transfers between devices, exchanged(): return [lax.ppermute(sends[0], 'freq', up + down)]  5.11 us
    ppermute x2, waiting for transfers between devices, exchanged(): return [lax.ppermute(sends[0], 'freq', up + down)]  1.36 us
  transfers between devices with their start and end apart: 2, of which 1 were waited for; matrix products, arithmetic and copies ran while one was open for 0% of the time, Pallas kernels for 11%

profile of v3, /device:TPU:0, one launch (start us, length us, event | category | flops | bytes accessed | tf_op | source)
XLA Modules:
  0.0 26.2 jit_solution(4758830406654540849)
XLA Ops:
  0.6 0.0 copy-start.3
  0.6 0.0 copy-start
  0.7 0.0 copy-start.1
  0.7 0.0 copy-start.2
  0.7 0.0 copy-start.4
  0.7 0.0 copy-start.5
  0.7 1.5 %shard_map.77.refs_1_ = f32[2,8,2,512]{3,2,1,0:T(2,128)S(1)} custom-call(f32[8,4,2,512]{3,2,1,0:T(2,128)} %refs_2_.1, f32[8,4,2,512]{3,2,1,0:T(2,128)} %b_ref.1, f32[8,4,2,16,512]{4,3,2,1,0:T(8,128)} %refs_3_.3, f32[8,4,16]{2,1,0:T(4,128)} %refs_4_.3, f32[1,512]{1,0:T(1,128)} %bitcast.14, f32[1,512]{1,0:T(1,128)} %bitcast.6), custom_call_target="tpu_custom_call" | custom-call | tf_op jit(solution)/shard_map/pallas_call | solution.py:38
  2.2 3.0 %collective-permute-start = (f32[2,8,2,512]{3,2,1,0:T(2,128)S(1)}, f32[2,8,2,512]{3,2,1,0:T(2,128)S(1)}, u32[]{:S(2)}, u32[]{:S(2)}) collective-permute-start(f32[2,8,2,512]{3,2,1,0:T(2,128)S(1)} %shard_map.77.refs_1_), channel_id=1, source_target_pairs={{0,1},{1,0},{2,3},{3,2},{4,5},{5,4},{6,7},{7,6},{8,9},{9,8},{10,11... | collective-permute-start | bytes 196616 | tf_op jit(solution)/shard_map/ppermute | solution.py:63
  5.3 0.0 copy-done.3
  5.3 0.0 copy-done
  5.3 0.0 copy-done.1
  5.3 0.0 copy-done.2
  5.3 0.0 copy-done.4
  5.3 0.0 copy-done.5
  5.3 0.8 %shard_map.78.refs_2_ = f32[8,4,2,512]{3,2,1,0:T(2,128)S(1)} custom-call(f32[8,4,2,512]{3,2,1,0:T(2,128)S(1)} %copy-done.1, f32[8,4,2,512]{3,2,1,0:T(2,128)S(1)} %copy-done.2, f32[8,4,2,16,512]{4,3,2,1,0:T(8,128)S(1)} %copy-done, f32[8,4,16]{2,1,0:T(4,128)S(1)} %copy-done.3, f32[1,512]{1,0:T(1,128)S(1)} %bitcast.15, f32[1,512]{1,0:T(1,128)S(1)} %bitcast.7), custom_call_target="tpu_custom_call" | custom-call | tf_op jit(solution)/shard_map/pallas_call | solution.py:38
  6.2 1.4 %collective-permute-done.refs_0_ = f32[2,8,2,512]{3,2,1,0:T(2,128)S(1)} collective-permute-done((f32[2,8,2,512]{3,2,1,0:T(2,128)S(1)}, f32[2,8,2,512]{3,2,1,0:T(2,128)S(1)}, u32[]{:S(2)}, u32[]{:S(2)}) %collective-permute-start) | collective-permute-done | bytes 65568 | tf_op jit(solution)/shard_map/ppermute | solution.py:63
  7.5 0.3 %shard_map.79 = (f32[8,2,512]{2,1,0:T(2,128)S(1)}, f32[8,2,512]{2,1,0:T(2,128)S(1)}) custom-call(f32[2,8,2,512]{3,2,1,0:T(2,128)S(1)} %collective-permute-done.refs_0_, f32[2,8,2,512]{3,2,1,0:T(2,128)S(1)} %shard_map.77.refs_1_, f32[8,4,2,512]{3,2,1,0:T(2,128)S(1)} %shard_map.78.refs_2_, f32[8,4,2,16,512]{4,3,2,1,0:T(8,128)S(1)} %copy-done, ...), custom_call_target="tpu_custom_call" | custom-call | tf_op jit(solution)/shard_map/pallas_call | solution.py:38
  7.8 2.1 %collective-permute-start.1 = (f32[8,2,512]{2,1,0:T(2,128)S(1)}, f32[8,2,512]{2,1,0:T(2,128)S(1)}, u32[]{:S(2)}, u32[]{:S(2)}) collective-permute-start(f32[8,2,512]{2,1,0:T(2,128)S(1)} %get-tuple-element.8.refs_1_), channel_id=1, source_target_pairs={{0,1},{1,0},{2,3},{3,2},{4,5},{5,4},{6,7},{7,6},{8,9},{9,8},{10,11... | collective-permute-start | bytes 98312 | tf_op jit(solution)/shard_map/ppermute | solution.py:63
  9.9 1.9 %shard_map.80 = (f32[8,4,2,512]{3,2,1,0:T(2,128)S(1)}, f32[8,4,2,512]{3,2,1,0:T(2,128)S(1)}, f32[8,4,2,512]{3,2,1,0:T(2,128)S(1)}, f32[1,128]{1,0:T(1,128)S(1)}) custom-call(f32[8,2,512]{2,1,0:T(2,128)S(1)} %get-tuple-element.9.refs_0_, f32[8,2,512]{2,1,0:T(2,128)S(1)} %get-tuple-element.8.refs_1_, f32[8,4,2,512]{3,2,1,0:T(2,128)S(1)} %shard_map.78.refs_2_, ...), custom_call_target="tpu_custom_call" | custom-call | tf_op jit(solution)/shard_map/pallas_call | solution.py:38
  11.8 0.0 collective-permute-done.1.refs_0_
  11.8 0.1 shard_map.81
  12.0 13.4 %all_to_all.11 = f32[32,1,128]{2,1,0:T(1,128)S(1)} all-to-all(f32[32,1,128]{2,1,0:T(1,128)S(1)} %bitcast.13), channel_id=1, replica_groups=mesh['ma'=16,'freq'=2] {'ma','freq'}, dimensions={0} | all-to-all | bytes 32768 | tf_op jit(solution)/shard_map/all_to_all | solution.py:256
  25.4 0.8 %shard_map.82 = (f32[8,4,2,512]{3,2,1,0:T(2,128)}, f32[8,4,2,512]{3,2,1,0:T(2,128)}) custom-call(f32[8,2,512]{2,1,0:T(2,128)S(1)} %collective-permute-done.1.refs_0_, f32[32,128]{1,0:T(8,128)S(1)} %bitcast.12, f32[8,4,2,512]{3,2,1,0:T(2,128)S(1)} %copy-done.1, f32[8,4,2,512]{3,2,1,0:T(2,128)S(1)} %get-tuple-element.11.refs_3_, ...), custom_call_target="tpu_custom_call" | custom-call | tf_op jit(solution)/shard_map/pallas_call | solution.py:38
Async XLA Ops:
  0.6 4.6 %copy-start.3 = (f32[8,4,16]{2,1,0:T(4,128)S(1)}, f32[8,4,16]{2,1,0:T(4,128)}, u32[]{:S(2)}) copy-start(f32[8,4,16]{2,1,0:T(4,128)} %refs_4_.3) | copy-start | bytes 6148
  0.6 4.6 %copy-start = (f32[8,4,2,16,512]{4,3,2,1,0:T(8,128)S(1)}, f32[8,4,2,16,512]{4,3,2,1,0:T(8,128)}, u32[]{:S(2)}) copy-start(f32[8,4,2,16,512]{4,3,2,1,0:T(8,128)} %refs_3_.3) | copy-start | bytes 6291460
  0.7 4.6 %copy-start.1 = (f32[8,4,2,512]{3,2,1,0:T(2,128)S(1)}, f32[8,4,2,512]{3,2,1,0:T(2,128)}, u32[]{:S(2)}) copy-start(f32[8,4,2,512]{3,2,1,0:T(2,128)} %refs_2_.1) | copy-start | bytes 393220
  0.7 4.6 %copy-start.2 = (f32[8,4,2,512]{3,2,1,0:T(2,128)S(1)}, f32[8,4,2,512]{3,2,1,0:T(2,128)}, u32[]{:S(2)}) copy-start(f32[8,4,2,512]{3,2,1,0:T(2,128)} %b_ref.1) | copy-start | bytes 393220
  0.7 4.6 %copy-start.4 = (f32[512]{0:T(512)S(1)}, f32[512]{0:T(512)}, u32[]{:S(2)}) copy-start(f32[512]{0:T(512)} %param.11) | copy-start | bytes 6148
  0.7 4.6 %copy-start.5 = (f32[512]{0:T(512)S(1)}, f32[512]{0:T(512)}, u32[]{:S(2)}) copy-start(f32[512]{0:T(512)} %param.10) | copy-start | bytes 6148
  2.2 5.3 %collective-permute-start = (f32[2,8,2,512]{3,2,1,0:T(2,128)S(1)}, f32[2,8,2,512]{3,2,1,0:T(2,128)S(1)}, u32[]{:S(2)}, u32[]{:S(2)}) collective-permute-start(f32[2,8,2,512]{3,2,1,0:T(2,128)S(1)} %shard_map.77.refs_1_), channel_id=1, source_target_pairs={{0,1},{1,0},{2,3},{3,2},{4,5},{5,4},{6,7},{7,6},{8,9},{9,8},{10,11... | collective-permute-start | bytes 196616 | tf_op jit(solution)/shard_map/ppermute | solution.py:63
  7.8 4.0 %collective-permute-start.1 = (f32[8,2,512]{2,1,0:T(2,128)S(1)}, f32[8,2,512]{2,1,0:T(2,128)S(1)}, u32[]{:S(2)}, u32[]{:S(2)}) collective-permute-start(f32[8,2,512]{2,1,0:T(2,128)S(1)} %get-tuple-element.8.refs_1_), channel_id=1, source_target_pairs={{0,1},{1,0},{2,3},{3,2},{4,5},{5,4},{6,7},{7,6},{8,9},{9,8},{10,11... | collective-permute-start | bytes 98312 | tf_op jit(solution)/shard_map/ppermute | solution.py:63

commit v4 on v3

--- a/solution.py
+++ b/solution.py
@@ -50,6 +50,8 @@
     ways = 1 if pair else 2
     ends = [0] if pair else [0, length - 1]
     inner = [j for j in range(length) if j not in ends]
+    half = modes // 2
+    parts = [(0, half), (half, modes)] if half else [(0, modes)]
     field = jax.ShapeDtypeStruct(right_side.shape, jnp.float32)
     edge = jax.ShapeDtypeStruct((modes, 2, width), jnp.float32)
     edge_pair = jax.ShapeDtypeStruct((2, modes, 2, width), jnp.float32)
@@ -106,10 +108,14 @@
         send_refs, refs = refs[:ways], refs[ways:]
         x_ref, b_ref, beam_ref, noise_ref, inv_ref, smooth_ref, sems = refs
         order, weights, _ = place()
-        copies = [(beam_hbm.at[:, order[j]], beam_ref.at[k]) for k, j in enumerate(ends)]
+        copies = [
+            (x_hbm, x_ref), (noise_hbm, noise_ref), (inv_hbm, inv_ref), (smooth_hbm, smooth_ref)
+        ]
         copies += [(b_hbm.at[:, order[j]], b_ref.at[k]) for k, j in enumerate(ends)]
         copies += [
-            (x_hbm, x_ref), (noise_hbm, noise_ref), (inv_hbm, inv_ref), (smooth_hbm, smooth_ref)
+            (beam_hbm.at[low:high, order[j]], beam_ref.at[k, low:high])
+            for low, high in parts
+            for k, j in enumerate(ends)
         ]
         copies = [
             pltpu.make_async_copy(source, target, sems.at[i])
@@ -117,7 +123,7 @@
         ]
         for copy in copies:
             copy.start()
-        for copy in copies:
+        for copy in copies[: 4 + ways]:
             copy.wait()
         inv, strength = inv_ref[...], smooth_ref[...]
 
@@ -133,8 +139,12 @@
                 send_refs[k][1, m] = b_ref[k, m] - apply(rows, j)
             return 0
 
-        lax.fori_loop(0, modes, step, 0, unroll=True)
-
+        for i, (low, high) in enumerate(parts):
+            for copy in copies[4 + ways * (i + 1) : 4 + ways * (i + 2)]:
+                copy.wait()
+            lax.fori_loop(low, high, step, 0, unroll=True)
+
+    beam_hbm = pltpu.with_memory_space_constraint(beam, pltpu.HBM)
     loads = (start_field, right_side, beam, noise, inv_power, smooth)
     scratch = [
         start_field.shape,
@@ -150,12 +160,18 @@
         *[pltpu.with_memory_space_constraint(array, pltpu.HBM) for array in loads],
         in_specs=[pl.BlockSpec(memory_space=pltpu.HBM)] * len(loads),
         scratch_shapes=[pltpu.VMEM(shape, jnp.float32) for shape in scratch]
-        + [pltpu.SemaphoreType.DMA((2 * ways + 4,))],
+        + [pltpu.SemaphoreType.DMA((4 + ways * (1 + len(parts)),))],
     )
     sends = list(sends)
     halos = exchanged(sends)
 
-    def middle(x_ref, b_ref, beam_ref, noise_ref, inv_ref, smooth_ref, p_ref):
+    def middle(x_ref, b_ref, beam_hbm, noise_ref, inv_ref, smooth_ref, p_ref, beam_ref, sems):
+        copies = [
+            pltpu.make_async_copy(beam_hbm.at[low:high], beam_ref.at[low:high], sems.at[i])
+            for i, (low, high) in enumerate(parts)
+        ]
+        for copy in copies:
+            copy.start()
         order, weights, _ = place()
         inv, strength = inv_ref[...], smooth_ref[...]
 
@@ -166,9 +182,18 @@
                 p_ref[m, j] = b_ref[m, order[j]] - apply(rows, j)
             return 0
 
-        lax.fori_loop(0, modes, step, 0, unroll=2)
-
-    partial = call(middle, field, start_field, right_side, beam, noise, inv_power, smooth)
+        for copy, (low, high) in zip(copies, parts):
+            copy.wait()
+            lax.fori_loop(low, high, step, 0, unroll=2)
+
+    in_vmem = pl.BlockSpec(memory_space=pltpu.VMEM)
+    partial, beam = call(
+        middle,
+        (field, jax.ShapeDtypeStruct(beam.shape, jnp.float32)),
+        start_field, right_side, beam_hbm, noise, inv_power, smooth,
+        in_specs=[in_vmem] * 2 + [pl.BlockSpec(memory_space=pltpu.HBM)] + [in_vmem] * 3,
+        scratch_shapes=[pltpu.SemaphoreType.DMA((len(parts),))],
+    )
 
     def second(*refs):
         halo_refs, send_refs, refs = refs[:ways], refs[ways : 2 * ways], refs[2 * ways :]
@@ -257,7 +282,8 @@
 
     def last(*refs):
         far_refs, refs = refs[:ways], refs[ways:]
-        sums_ref, x_ref, r_ref, w_ref, z_ref, smooth_ref, out_ref, resid_ref = refs
+        sums_ref, x_ref, r_ref, w_ref, z_ref, smooth_ref = refs[:6]
+        out_hbm, resid_hbm, out_ref, resid_ref, sems = refs[6:]
         order, _, exists = place()
         total = jnp.sum(sums_ref[...], axis=0, keepdims=True)
         lane = lax.broadcasted_iota(jnp.int32, (1, LANES), 1)
@@ -274,14 +300,27 @@
         on_w = (step1 * step0).reshape(1, 1, 1, 1)
         r, w = r_ref[...], w_ref[...]
         out_ref[...] = x_ref[...] + on_r * r - on_w * w
+        out_copy = pltpu.make_async_copy(out_ref, out_hbm, sems.at[0])
+        out_copy.start()
         resid_ref[...] = r - on_r * w + on_w * z_ref[...]
         scale = (step1 * step0).reshape(1, 1, 1) * smooth_ref[...].reshape(1, 1, width)
         for far, j, there in zip(far_refs, ends, exists):
             value = kept(there, scale * far[...])
             resid_ref[:, order[j]] = resid_ref[:, order[j]] - value
+        resid_copy = pltpu.make_async_copy(resid_ref, resid_hbm, sems.at[1])
+        resid_copy.start()
+        out_copy.wait()
+        resid_copy.wait()
 
     return tuple(
-        call(last, (field, field), *far_ends, sums, start_field, resid, along, twice, smooth)
+        call(
+            last,
+            (field, field),
+            *far_ends, sums, start_field, resid, along, twice, smooth,
+            out_specs=(pl.BlockSpec(memory_space=pltpu.HBM),) * 2,
+            scratch_shapes=[pltpu.VMEM(field.shape, jnp.float32)] * 2
+            + [pltpu.SemaphoreType.DMA((2,))],
+        )
     )
 
 

time: 26.3 us -> 26.4 us (level)
  waiting for transfers between devices: 1.36 us -> 0.14 us
  Pallas kernels: 5.58 us -> 6.8 us
    pallas_call x6, Pallas kernels: 5.58 us -> 6.8 us  [call(): pl.pallas_call(body, out_shape=outs, compiler_params=pltpu.CompilerParams...]
    ppermute x2, waiting for transfers between devices: 1.36 us -> 0.14 us  [exchanged(): return [lax.ppermute(sends[0], 'freq', up + down)]]
  transfers between devices with their start and end apart: 2 -> 2, of which waited for: 1 -> 1; matrix products, arithmetic and copies ran while one was open for 0% -> 0% of each run, Pallas kernels for 11% -> 15%
where the time goes in v4:
time: 26.4 us; the launch traced here: 26.2 us
  blocking collectives  13.4 us (51%)
  Pallas kernels  6.8 us (26%)
  starting transfers between devices  5.11 us (19%)
  between operations  0.72 us (3%)
    all_to_all x1, blocking collectives, shards(): sums = lax.all_to_all(sums, AXES, 0, 0, tiled=True)  13.4 us
    pallas_call x6, Pallas kernels, call(): pl.pallas_call(body, out_shape=outs, compiler_params=pltpu.CompilerParams...  6.8 us
    ppermute x2, starting transfers between devices, exchanged(): return [lax.ppermute(sends[0], 'freq', up + down)]  5.11 us
  transfers between devices with their start and end apart: 2, of which 1 were waited for; matrix products, arithmetic and copies ran while one was open for 0% of the time, Pallas kernels for 15%

profile of v4, /device:TPU:0, one launch (start us, length us, event | category | flops | bytes accessed | tf_op | source)
XLA Modules:
  0.0 26.2 jit_solution(8803865970709688514)
XLA Ops:
  0.6 0.0 copy-start.2
  0.6 0.0 copy-start
  0.7 0.0 copy-start.1
  0.7 0.0 copy-start.3
  0.7 0.0 copy-start.4
  0.7 1.5 %shard_map.77.refs_1_ = f32[2,8,2,512]{3,2,1,0:T(2,128)S(1)} custom-call(f32[8,4,2,512]{3,2,1,0:T(2,128)} %refs_2_.1, f32[8,4,2,512]{3,2,1,0:T(2,128)} %b_ref.1, f32[8,4,2,16,512]{4,3,2,1,0:T(8,128)} %beam_hbm.3, f32[8,4,16]{2,1,0:T(4,128)} %refs_4_.3, f32[1,512]{1,0:T(1,128)} %bitcast.14, f32[1,512]{1,0:T(1,128)} %bitcast.6), custom_call_target="tpu_custom_call" | custom-call | tf_op jit(solution)/shard_map/pallas_call | solution.py:38
  2.2 3.0 %collective-permute-start = (f32[2,8,2,512]{3,2,1,0:T(2,128)S(1)}, f32[2,8,2,512]{3,2,1,0:T(2,128)S(1)}, u32[]{:S(2)}, u32[]{:S(2)}) collective-permute-start(f32[2,8,2,512]{3,2,1,0:T(2,128)S(1)} %shard_map.77.refs_1_), channel_id=1, source_target_pairs={{0,1},{1,0},{2,3},{3,2},{4,5},{5,4},{6,7},{7,6},{8,9},{9,8},{10,11... | collective-permute-start | bytes 196616 | tf_op jit(solution)/shard_map/ppermute | solution.py:65
  5.2 0.0 copy-done.2
  5.2 0.0 copy-done
  5.2 0.0 copy-done.1
  5.2 0.0 copy-done.3
  5.3 0.0 copy-done.4
  5.3 2.1 %shard_map.78 = (f32[8,4,2,512]{3,2,1,0:T(2,128)S(1)}, f32[8,4,2,16,512]{4,3,2,1,0:T(8,128)S(1)}) custom-call(f32[8,4,2,512]{3,2,1,0:T(2,128)S(1)} %copy-done, f32[8,4,2,512]{3,2,1,0:T(2,128)S(1)} %copy-done.1, f32[8,4,2,16,512]{4,3,2,1,0:T(8,128)} %beam_hbm.3, f32[8,4,16]{2,1,0:T(4,128)S(1)} %copy-done.2, f32[1,512]{1,0:T(1,128)S(1)} %bitcast.15, ...), custom_call_target="tpu_custom_call" | custom-call | tf_op jit(solution)/shard_map/pallas_call | solution.py:38
  7.3 0.1 collective-permute-done.refs_0_
  7.5 0.3 %shard_map.79 = (f32[8,2,512]{2,1,0:T(2,128)S(1)}, f32[8,2,512]{2,1,0:T(2,128)S(1)}) custom-call(f32[2,8,2,512]{3,2,1,0:T(2,128)S(1)} %collective-permute-done.refs_0_, f32[2,8,2,512]{3,2,1,0:T(2,128)S(1)} %shard_map.77.refs_1_, f32[8,4,2,512]{3,2,1,0:T(2,128)S(1)} %get-tuple-element.10.refs_2_, f32[8,4,2,16,512]{4,3,2,1,0:T(8,128)S(1)} %get-tuple-element.11.refs_3_, ...), custom_call_target="tpu_custom_call" | custom-call | tf_op jit(solution)/shard_map/pallas_call | solution.py:38
  7.8 2.1 %collective-permute-start.1 = (f32[8,2,512]{2,1,0:T(2,128)S(1)}, f32[8,2,512]{2,1,0:T(2,128)S(1)}, u32[]{:S(2)}, u32[]{:S(2)}) collective-permute-start(f32[8,2,512]{2,1,0:T(2,128)S(1)} %get-tuple-element.12.refs_1_), channel_id=1, source_target_pairs={{0,1},{1,0},{2,3},{3,2},{4,5},{5,4},{6,7},{7,6},{8,9},{9,8},{10,11... | collective-permute-start | bytes 98312 | tf_op jit(solution)/shard_map/ppermute | solution.py:65
  9.9 1.9 %shard_map.80 = (f32[8,4,2,512]{3,2,1,0:T(2,128)S(1)}, f32[8,4,2,512]{3,2,1,0:T(2,128)S(1)}, f32[8,4,2,512]{3,2,1,0:T(2,128)S(1)}, f32[1,128]{1,0:T(1,128)S(1)}) custom-call(f32[8,2,512]{2,1,0:T(2,128)S(1)} %get-tuple-element.13.refs_0_, f32[8,2,512]{2,1,0:T(2,128)S(1)} %get-tuple-element.12.refs_1_, f32[8,4,2,512]{3,2,1,0:T(2,128)S(1)} %get-tuple-element.10.refs_2_, ...), custom_call_target="tpu_custom_call" | custom-call | tf_op jit(solution)/shard_map/pallas_call | solution.py:38
  11.8 0.0 collective-permute-done.1.refs_0_
  11.8 0.1 shard_map.81
  12.0 13.4 %all_to_all.11 = f32[32,1,128]{2,1,0:T(1,128)S(1)} all-to-all(f32[32,1,128]{2,1,0:T(1,128)S(1)} %bitcast.13), channel_id=1, replica_groups=mesh['ma'=16,'freq'=2] {'ma','freq'}, dimensions={0} | all-to-all | bytes 32768 | tf_op jit(solution)/shard_map/all_to_all | solution.py:281
  25.3 0.8 %shard_map.82 = (f32[8,4,2,512]{3,2,1,0:T(2,128)}, f32[8,4,2,512]{3,2,1,0:T(2,128)}) custom-call(f32[8,2,512]{2,1,0:T(2,128)S(1)} %collective-permute-done.1.refs_0_, f32[32,128]{1,0:T(8,128)S(1)} %bitcast.12, f32[8,4,2,512]{3,2,1,0:T(2,128)S(1)} %copy-done, f32[8,4,2,512]{3,2,1,0:T(2,128)S(1)} %get-tuple-element.15.refs_3_, ...), custom_call_target="tpu_custom_call" | custom-call | tf_op jit(solution)/shard_map/pallas_call | solution.py:38
Async XLA Ops:
  0.6 4.6 %copy-start.2 = (f32[8,4,16]{2,1,0:T(4,128)S(1)}, f32[8,4,16]{2,1,0:T(4,128)}, u32[]{:S(2)}) copy-start(f32[8,4,16]{2,1,0:T(4,128)} %refs_4_.3) | copy-start | bytes 6148
  0.6 4.6 %copy-start = (f32[8,4,2,512]{3,2,1,0:T(2,128)S(1)}, f32[8,4,2,512]{3,2,1,0:T(2,128)}, u32[]{:S(2)}) copy-start(f32[8,4,2,512]{3,2,1,0:T(2,128)} %refs_2_.1) | copy-start | bytes 393220
  0.7 4.6 %copy-start.1 = (f32[8,4,2,512]{3,2,1,0:T(2,128)S(1)}, f32[8,4,2,512]{3,2,1,0:T(2,128)}, u32[]{:S(2)}) copy-start(f32[8,4,2,512]{3,2,1,0:T(2,128)} %b_ref.1) | copy-start | bytes 393220
  0.7 4.6 %copy-start.3 = (f32[512]{0:T(512)S(1)}, f32[512]{0:T(512)}, u32[]{:S(2)}) copy-start(f32[512]{0:T(512)} %param.11) | copy-start | bytes 6148
  0.7 4.6 %copy-start.4 = (f32[512]{0:T(512)S(1)}, f32[512]{0:T(512)}, u32[]{:S(2)}) copy-start(f32[512]{0:T(512)} %param.10) | copy-start | bytes 6148
  2.2 5.3 %collective-permute-start = (f32[2,8,2,512]{3,2,1,0:T(2,128)S(1)}, f32[2,8,2,512]{3,2,1,0:T(2,128)S(1)}, u32[]{:S(2)}, u32[]{:S(2)}) collective-permute-start(f32[2,8,2,512]{3,2,1,0:T(2,128)S(1)} %shard_map.77.refs_1_), channel_id=1, source_target_pairs={{0,1},{1,0},{2,3},{3,2},{4,5},{5,4},{6,7},{7,6},{8,9},{9,8},{10,11... | collective-permute-start | bytes 196616 | tf_op jit(solution)/shard_map/ppermute | solution.py:65
  7.8 4.0 %collective-permute-start.1 = (f32[8,2,512]{2,1,0:T(2,128)S(1)}, f32[8,2,512]{2,1,0:T(2,128)S(1)}, u32[]{:S(2)}, u32[]{:S(2)}) collective-permute-start(f32[8,2,512]{2,1,0:T(2,128)S(1)} %get-tuple-element.12.refs_1_), channel_id=1, source_target_pairs={{0,1},{1,0},{2,3},{3,2},{4,5},{5,4},{6,7},{7,6},{8,9},{9,8},{10,11... | collective-permute-start | bytes 98312 | tf_op jit(solution)/shard_map/ppermute | solution.py:65
